TPU v7x, 256 devices: a whole 4x4x8 slice. The times are simulated.
256 devices in a mesh: seq: 32 (over y, z), tp: 8 (over x, core).
Axes of the slice: x: 4, y: 4, z: 8, core: 2. Of those that a mesh axis runs over, the one named last changes fastest.
Arguments:
- tokens: bfloat16 [24576, 2048], P('seq', 'tp'), may hold values from -20 to 20
- w_query: bfloat16 [2048, 2048], P(None, 'tp'), may hold values from -0.125 to 0.125
- w_key: bfloat16 [2048, 2048], P(None, 'tp'), may hold values from -0.125 to 0.125
- w_value: bfloat16 [2048, 2048], P(None, 'tp'), may hold values from -0.125 to 0.125
- head_gain: float32 [2048], P('tp'), may hold values from 0.5 to 1.5
- w_out: bfloat16 [2048, 2048], P('tp'), may hold values from -0.125 to 0.125
- norm_gain: float32 [2048], replicated, may hold values from 0.5 to 1.5
- w_gate: bfloat16 [2048, 8192], P('seq', 'tp'), may hold values from -0.125 to 0.125
- w_up: bfloat16 [2048, 8192], P('seq', 'tp'), may hold values from -0.125 to 0.125
- w_down: bfloat16 [8192, 2048], P('tp', 'seq'), may hold values from -0.0625 to 0.0625
Outputs:
- layer_out: bfloat16 [24576, 2048], P('seq', 'tp')
All inputs are finite; a program needn't handle non-finite values.
Results may differ from a plain program's by a relative error of at most 0.009.
Values may be sent and summed in bfloat16 or wider, within the bound.
No kernel may reach another device: no remote copies, remote signals or barrier semaphores. Data moves between devices by JAX's collectives and lax.ppermute only.
A program may use at most 128 MiB of HBM per device.

v0:
```python
import jax
import jax.numpy as jnp
from jax import lax
from jax.sharding import Mesh
from jax.sharding import PartitionSpec as P

HD = 128
SEQ = ("seq_0", "seq_1")


def nothing_yet(array, identity):
    return jnp.zeros_like(array) + jnp.asarray(identity, array.dtype)


def entering(array, axes, combine, identity):
    before = start = nothing_yet(array, identity)
    total = array
    for axis in reversed(axes):
        peers, position = (lax.axis_size(axis), lax.axis_index(axis))
        pieces = lax.all_gather(total.astype(jnp.bfloat16), axis)
        inside, total = (start, start)
        for k in range(peers):
            passed = k < position
            total = combine(total, pieces[k].astype(array.dtype))
            inside = jnp.where(passed, total, inside)
        before = combine(inside, before)
    return before


def in_one_piece(arrays, axis, dim, along):
    ends, at = ([], 0)
    for a in arrays[:-1]:
        at += a.shape[along]
        ends.append(at)
    both = jnp.concatenate(arrays, axis=along)
    return tuple(jnp.split(lax.all_gather(both, axis, axis=dim, tiled=True), ends, axis=along))


def split_up(array, dim, peers):
    shape = array.shape
    tiles = array.reshape(*shape[:dim], peers, shape[dim] // peers, *shape[dim + 1 :])
    return jnp.moveaxis(tiles, dim, 0)


def sum_at_owner(array, axis, dim):
    tiles = split_up(array, dim, lax.axis_size(axis))
    arrived = lax.all_to_all(tiles, axis, split_axis=0, concat_axis=0, tiled=True)
    return arrived.astype(jnp.float32).sum(axis=0)


def add_states(earlier, later):
    return earlier + later


def body(tokens, w_query, w_key, w_value, head_gain, w_out, norm_gain, w_gate, w_up, w_down):
    length = tokens.shape[0]
    width_here = tokens.shape[1]
    heads_here = w_query.shape[1] // HD
    features = lax.all_gather(tokens, "tp", axis=1, tiled=True)

    def project(weight):
        product = jnp.dot(features, weight, preferred_element_type=jnp.float32)
        return product.astype(jnp.bfloat16).reshape(length, heads_here, HD)

    query = project(w_query)
    keys_local = project(w_key)
    values_local = project(w_value)
    scores = jnp.einsum("ihd,jhd->hij", query, keys_local, preferred_element_type=jnp.float32)
    causal = jnp.arange(length)[:, None] >= jnp.arange(length)[None, :]
    scores = jnp.where(causal[None], scores, 0.0).astype(jnp.bfloat16)
    inside = jnp.einsum("hij,jhd->ihd", scores, values_local, preferred_element_type=jnp.float32)
    own_state = jnp.einsum(
        "jhd,jhe->hde", keys_local, values_local, preferred_element_type=jnp.float32
    )
    history = entering(own_state, SEQ, add_states, jnp.zeros_like(own_state))
    carried = jnp.einsum(
        "ihd,hde->ihe", query, history.astype(jnp.bfloat16), preferred_element_type=jnp.float32
    )
    mixed = inside + carried
    scale = lax.rsqrt(jnp.mean(mixed * mixed, axis=-1, keepdims=True) + 1e-06)
    normed = (mixed * scale * head_gain.reshape(heads_here, HD)).astype(jnp.bfloat16)
    normed = normed.reshape(length, heads_here * HD)
    partial_value = jnp.dot(normed, w_out, preferred_element_type=jnp.float32)
    own_column = lax.axis_index("tp") * width_here
    summed = lax.psum(partial_value.astype(jnp.bfloat16), "tp").astype(jnp.float32)
    resid_whole = features.astype(jnp.float32) + summed
    factor = lax.rsqrt(jnp.mean(resid_whole * resid_whole, axis=-1, keepdims=True) + 1e-05)
    ffn_in = (resid_whole * factor * norm_gain).astype(jnp.bfloat16)
    resid = lax.dynamic_slice_in_dim(resid_whole, own_column, width_here, 1)
    pieces = in_one_piece((w_gate, w_up), SEQ, 0, 1)
    gate_sum = jnp.dot(ffn_in, pieces[0], preferred_element_type=jnp.float32)
    upward_sum = jnp.dot(ffn_in, pieces[1], preferred_element_type=jnp.float32)
    hidden = (jax.nn.silu(gate_sum) * upward_sum).astype(jnp.bfloat16)
    terms = jnp.dot(
        hidden, lax.all_gather(w_down, SEQ, axis=1, tiled=True), preferred_element_type=jnp.float32
    )
    mlp_share = sum_at_owner(terms.astype(jnp.bfloat16), "tp", 1)
    return (resid + mlp_share).astype(jnp.bfloat16)


def solution(mesh):
    finer = Mesh(mesh.devices.reshape(4, 8, mesh.shape["tp"]), ("seq_0", "seq_1", "tp"))
    return jax.shard_map(
        body,
        mesh=finer,
        in_specs=(
            P(SEQ, "tp"),
            P(None, "tp"),
            P(None, "tp"),
            P(None, "tp"),
            P("tp"),
            P("tp", None),
            P(),
            P(SEQ, "tp"),
            P(SEQ, "tp"),
            P("tp", SEQ),
        ),
        out_specs=P(SEQ, "tp"),
        check_vma=False,
    )
```

profile of v0, /device:TPU:1, one launch (start us, length us, event | category | flops | bytes accessed | tf_op | source)
XLA Modules:
  0.0 356.1 jit_solution(3774338087254047791)
XLA Ops:
  7.4 0.7 all-gather.5.cloned.1.call-update
  8.2 0.2 iota_compare_fusion
  8.3 39.5 %all-gather.5.cloned.1.call-done = bf16[768,2048]{1,0:T(8,128)(2,1)} async-done(((bf16[768,256]{1,0:T(8,128)(2,1)}), bf16[768,2048]{1,0:T(8,128)(2,1)}) %all-gather.5.cloned.1.call-update) | async-done | bytes 3145744 | tf_op jit(solution)/shard_map/all_gather | solution.py:59
  47.9 3.3 convolution_convert_fusion.2
  51.2 2.4 convolution_convert_fusion.4
  53.6 0.3 convolution_convert_fusion.5
  53.9 20.8 %all-gather = bf16[16,128,128]{2,1,0:T(8,128)(2,1)S(1)} all-gather(bf16[2,128,128]{2,1,0:T(8,128)(2,1)S(1)} %convolution_convert_fusion.5), channel_id=2, replica_groups=mesh['seq_0'=4,'seq_1'=8,'tp'=8] {'seq_1'}, dimensions={0}, use_global_device_ids=true | all-gather | bytes 589824 | tf_op jit(solution)/shard_map/all_gather | solution.py:20
  74.7 0.1 fusion.28
  74.7 9.7 %all_gather.22 = bf16[4,2,128,128]{3,2,1,0:T(8,128)(2,1)S(1)} all-gather(bf16[1,2,128,128]{3,2,1,0:T(8,128)(2,1)S(1)} %fusion.28), channel_id=1, replica_groups=mesh['seq_0'=4,'seq_1'=8,'tp'=8] {'seq_0'}, dimensions={0}, use_global_device_ids=true | all-gather | bytes 327680 | tf_op jit(solution)/shard_map/all_gather | solution.py:20
  84.5 1.1 convolution_convert_fusion.3
  85.6 0.7 copy-done.7
  86.3 1.3 fusion.29
  87.6 2.9 multiply_reduce_fusion.1
  90.5 0.1 multiply_convert_fusion.2
  90.6 2.7 convolution_convert_fusion.1
  93.4 0.0 all-gather.7.cloned.1.call-start
  93.5 0.8 copy-done.2
  94.3 0.1 copy-done.3
  94.3 0.7 pad_maximum_fusion
  95.1 0.2 all-gather.9.cloned.1.call-start
  95.3 0.4 all-gather.9.cloned.1.call-update
  95.7 79.1 %all-reduce.2.cloned.1.call-done = bf16[768,2048]{1,0:T(8,128)(2,1)} async-done(((bf16[768,2048]{1,0:T(8,128)(2,1)}), bf16[768,2048]{1,0:T(8,128)(2,1)}) %all-reduce.2.cloned.1.call-update) | async-done | bytes 3145744 | tf_op jit(solution)/shard_map/psum | solution.py:85
  174.8 6.7 %convert_add_fusion = (f32[768,2048]{1,0:T(8,128)}, f32[768]{0:T(1024)S(1)}) fusion(bf16[768,2048]{1,0:T(8,128)(2,1)} %all-reduce.2.cloned.1.call-done, bf16[768,2048]{1,0:T(8,128)(2,1)} %all-gather.5.cloned.1.call-done), kind=kLoop, calls=%fused_computation.3 | loop fusion | flops 7863552 | bytes 12585984 | tf_op jit(solution)/shard_map/add | solution.py:86
  181.6 19.3 %all-gather.7.cloned.1.call-done = bf16[2048,2048]{1,0:T(8,128)(2,1)} async-done(((bf16[64,2048]{1,0:T(8,128)(2,1)}), bf16[2048,2048]{1,0:T(8,128)(2,1)}) %all-gather.7.cloned.1.call-update) | async-done | bytes 8388624 | tf_op jit(solution)/shard_map/all_gather | solution.py:36
  200.9 9.2 %fusion = f32[768,1024]{1,0:T(8,128)} fusion(bf16[2048,2048]{1,0:T(8,128)(2,1)} %all-gather.7.cloned.1.call-done, f32[2048]{0:T(1024)S(1)} %copy-done.6, f32[768]{0:T(1024)S(1)} %add_rsqrt_fusion.1, bf16[768,2048]{1,0:T(8,128)(2,1)} %all-reduce.2.cloned.1.call-done, bf16[768,2048]{1,0:T(8,128)(2,1)} %all-gather.5.cloned.1.call-done), kind=kOutput, calls=%fused_computation.5 | convolution fusion | flops 3230662656 | bytes 13642752 | tf_op jit(solution)/shard_map/dot_general | solution.py:92
  210.2 69.3 %all-gather.9.cloned.1.call-done = bf16[1024,2048]{0,1:T(8,128)(2,1)} async-done(((bf16[1024,64]{0,1:T(8,128)(2,1)}), bf16[1024,2048]{0,1:T(8,128)(2,1)}) %all-gather.9.cloned.1.call-update) | async-done | bytes 4194320 | tf_op jit(solution)/shard_map/all_gather | solution.py:95
  279.5 14.9 %convolution_convert_fusion = bf16[768,2048]{1,0:T(8,128)(2,1)} fusion(bf16[1024,2048]{0,1:T(8,128)(2,1)} %all-gather.9.cloned.1.call-done, f32[768,1024]{1,0:T(8,128)} %fusion, bf16[2048,2048]{1,0:T(8,128)(2,1)} %all-gather.7.cloned.1.call-done, f32[2048]{0:T(1024)S(1)} %copy-done.6, f32[768]{0:T(1024)S(1)} %add_rsqrt_fusion.1, ...), kind=kOutput, calls=%fused_computation.9 | convolution fusion | flops 6458179584 | bytes 20982784 | tf_op jit(solution)/shard_map/dot_general | solution.py:94
  294.4 3.7 %copy.23 = bf16[96,8,8,256]{3,2,0,1:T(8,128)(2,1)} copy(bf16[96,8,8,256]{3,2,1,0:T(8,128)(2,1)} %bitcast.58) | data formatting | bytes 6291456 | tf_op jit(solution)/shard_map/reshape | solution.py:41
  298.1 8.6 %all-to-all-start = ((bf16[8,768,256]{2,1,0:T(8,128)(2,1)}), bf16[8,768,256]{2,1,0:T(8,128)(2,1)}, u32[]{:S(2)}, u32[]{:S(2)}) async-start(bf16[8,768,256]{2,1,0:T(8,128)(2,1)} %bitcast.57), calls=%async_computation | async-start | bytes 6291456 | tf_op jit(solution)/shard_map/all_to_all | solution.py:47
  306.7 37.6 %all-to-all-done = bf16[8,768,256]{2,1,0:T(8,128)(2,1)} async-done(((bf16[8,768,256]{2,1,0:T(8,128)(2,1)}), bf16[8,768,256]{2,1,0:T(8,128)(2,1)}, u32[]{:S(2)}, u32[]{:S(2)}) %all-to-all-start) | async-done | bytes 3145760 | tf_op jit(solution)/shard_map/all_to_all | solution.py:47
  344.3 2.4 convert_reduce_fusion
  346.7 2.0 add_convert_fusion
  (19 shorter events, 0.1 us)
Async XLA Ops:
  7.4 83.3 %copy-start = (bf16[256,2048]{1,0:T(8,128)(2,1)S(1)}, bf16[256,2048]{1,0:T(8,128)(2,1)}, u32[]{:S(2)}) copy-start(bf16[256,2048]{1,0:T(8,128)(2,1)} %param.15) | copy-start | bytes 3145732
  7.4 40.5 %all-gather.5.cloned.1.call-start = ((), (), s32[]{:S(2)}) async-start(), calls=%async_computation.1 | async-start | bytes 3538944 | tf_op jit(solution)/shard_map/all_gather | solution.py:59
  8.1 166.7 %all-reduce.2.cloned.1.call-start = ((), (), s32[]{:S(2)}) async-start(), calls=%async_computation.2 | async-start | bytes 6291456 | tf_op jit(solution)/shard_map/psum | solution.py:85
  47.9 3.4 copy-start.1
  51.2 33.2 %copy-start.5 = (bf16[2048,256]{1,0:T(8,128)(2,1)S(1)}, bf16[2048,256]{1,0:T(8,128)(2,1)}, u32[]{:S(2)}) copy-start(bf16[2048,256]{1,0:T(8,128)(2,1)} %param.11) | copy-start | bytes 3145732
  85.6 0.7 copy-start.7
  87.6 2.9 copy-start.4
  93.4 0.9 copy-start.2
  93.4 1.0 copy-start.3
  93.4 107.5 %all-gather.7.cloned.1.call-start = ((), (), s32[]{:S(2)}) async-start(), calls=%async_computation.3 | async-start | bytes 8650752 | tf_op jit(solution)/shard_map/all_gather | solution.py:36
  95.1 184.4 %all-gather.9.cloned.1.call-start = ((), (), s32[]{:S(2)}) async-start(), calls=%async_computation.4 | async-start | bytes 4325376 | tf_op jit(solution)/shard_map/all_gather | solution.py:95
  95.7 105.2 %copy-start.6 = (f32[2048]{0:T(1024)S(1)}, f32[2048]{0:T(1024)}, u32[]{:S(2)}) copy-start(f32[2048]{0:T(1024)} %param.16) | copy-start | bytes 24580
  298.1 46.2 %all-to-all-start = ((bf16[8,768,256]{2,1,0:T(8,128)(2,1)}), bf16[8,768,256]{2,1,0:T(8,128)(2,1)}, u32[]{:S(2)}, u32[]{:S(2)}) async-start(bf16[8,768,256]{2,1,0:T(8,128)(2,1)} %bitcast.57), calls=%async_computation | async-start | bytes 6291456 | tf_op jit(solution)/shard_map/all_to_all | solution.py:47
Sparse Core Ops, SparseCore 0:
  10.0 37.8 all-gather.4
  93.5 81.2 all-reduce.1
Sparse Core Ops, SparseCore 1:
  96.5 104.4 all-gather.6
  203.4 76.1 all-gather.8
where the time goes:
time: 356 us
  waiting for transfers between devices  246 us (69%)
  matrix products  38.1 us (11%)
  blocking collectives  30.5 us (9%)
  between operations  15 us (4%)
  other arithmetic  12.2 us (3%)
  starting transfers between devices  8.92 us (3%)
  local copies, waits for them, and re-layouts  5.37 us (2%)
    psum x1, waiting for transfers between devices, body(): lax.psum(partial_value.astype(jnp.bfloat16), 'tp').astype(jnp.float32)  79.1 us
    all_gather x1, waiting for transfers between devices, body(): lax.all_gather(w_down, SEQ, axis=1, tiled=True)  69.3 us
    all_gather x1, waiting for transfers between devices, body(): features = lax.all_gather(tokens, 'tp', axis=1, tiled=True)  39.5 us
    all_to_all x1, waiting for transfers between devices, sum_at_owner(): lax.all_to_all(tiles, axis, split_axis=0, concat_axis=0, tiled=True)  37.6 us
    all_gather x2, blocking collectives, entering(): pieces = lax.all_gather(total.astype(jnp.bfloat16), axis)  30.5 us
    all_gather x1, waiting for transfers between devices, in_one_piece(): lax.all_gather(both, axis, axis=dim, tiled=True)  19.3 us
    dot_general x1, matrix products, body(): jnp.dot(hidden, lax.all_gather(w_down, SEQ, axis=1, tiled=True), preferre...  14.9 us
    dot_general x1, matrix products, body(): upward_sum = jnp.dot(ffn_in, pieces[1], preferred_element_type=jnp.float32)  9.24 us
  transfers between devices with their start and end apart: 5, of which 5 were waited for; matrix products, arithmetic and copies ran while one was open for 5% of the time, Pallas kernels for 0%

commit v1 on v0

v1 whole, which is shorter than its diff:
```python
import functools

import jax
import jax.numpy as jnp
from jax import lax
from jax.experimental import pallas as pl
from jax.experimental.pallas import tpu as pltpu
from jax.sharding import Mesh
from jax.sharding import PartitionSpec as P


HD = 128
W = 256
SEQ = ("y", "z")
TP = ("x", "core")
BF = jnp.bfloat16
F32 = jnp.float32


def shift(a, axis, by):
    n = lax.axis_size(axis)
    return lax.ppermute(a, axis, [(i, (i + by) % n) for i in range(n)])


def swap(a):
    return shift(a, "core", 1)


def spread(t):
    mine, theirs = [t], []
    for d in (1, 2, 3):
        mine.append(shift(t, "x", d))
    for d in range(4):
        theirs.append(swap(mine[d]))
    return mine, theirs


def here(a):
    return pltpu.with_memory_space_constraint(a, pltpu.VMEM)


def kernel_of(body, out, *args, scratch=(), flops=0, grant=8):
    place = pl.BlockSpec(memory_space=pltpu.SMEM)
    vmem = pl.BlockSpec(memory_space=pltpu.VMEM)
    stays = pl.BlockSpec(memory_space=pltpu.HBM)
    specs, values = [], []
    for a in args:
        if isinstance(a, tuple):
            specs.append(stays)
            values.append(pltpu.with_memory_space_constraint(a[0], pltpu.HBM))
        elif a.dtype == jnp.int32:
            specs.append(place)
            values.append(a)
        else:
            specs.append(vmem)
            values.append(here(a))
    return pl.pallas_call(
        body,
        in_specs=specs,
        out_specs=[stays if space else vmem for _, _, *space in out],
        out_shape=[(space or [pltpu.VMEM])[0](shape, dtype) for shape, dtype, *space in out],
        scratch_shapes=list(scratch),
        compiler_params=pltpu.CompilerParams(vmem_limit_bytes=grant << 20),
        cost_estimate=pl.CostEstimate(flops=flops, bytes_accessed=8 << 20, transcendentals=0),
    )(*values)


def dot(a, b, dims=((1,), (0,))):
    return lax.dot_general(a, b, (dims, ((), ())), preferred_element_type=F32)


def pieces_of(place, mine, theirs):
    x, core = place[0], place[1]
    for d in range(4):
        chip = lax.rem(x + 4 - d, 4)
        yield pl.multiple_of((2 * chip + core) * W, W), mine[d]
        yield pl.multiple_of((2 * chip + 1 - core) * W, W), theirs[d]


def by_tiles(length, step):
    def run(i, _):
        step(pl.ds(pl.multiple_of(i * 256, 256), 256))
        return 0

    lax.fori_loop(0, length // 256, run, 0)


def keys_kernel(place, *refs):
    k_from, v_from, whole, keys, values, state, w_key, w_value, sems = refs[8:]
    load_k = pltpu.make_async_copy(k_from, w_key, sems.at[0])
    load_v = pltpu.make_async_copy(v_from, w_value, sems.at[1])
    load_k.start()
    load_v.start()

    @functools.partial(by_tiles, whole.shape[0])
    def _(rows):
        for at, piece in pieces_of(place, refs[:4], refs[4:8]):
            whole[rows, pl.ds(at, W)] = piece[rows, :]

    load_k.wait()
    load_v.wait()

    @functools.partial(by_tiles, whole.shape[0])
    def _(rows):
        keys[rows, :] = dot(whole[rows, :], w_key[...]).astype(BF)
        values[rows, :] = dot(whole[rows, :], w_value[...]).astype(BF)

    for h in range(2):
        cols = slice(h * HD, (h + 1) * HD)
        state[h] = dot(keys[:, cols], values[:, cols], ((0,), (0,))).astype(BF)


def query_kernel(whole, w_query, query):
    @functools.partial(by_tiles, whole.shape[0])
    def _(rows):
        query[rows, :] = dot(whole[rows, :], w_query[...]).astype(BF)


def inside_kernel(query, keys, values, inside):
    length = keys.shape[0]

    @functools.partial(by_tiles, length)
    def _(rows):
        i = lax.broadcasted_iota(jnp.int32, (256, length), 0) + rows.start
        j = lax.broadcasted_iota(jnp.int32, (256, length), 1)
        for h in range(2):
            cols = slice(h * HD, (h + 1) * HD)
            s = dot(query[rows, cols], keys[:, cols], ((1,), (1,)))
            s = jnp.where(i >= j, s, 0.0).astype(BF)
            inside[rows, cols] = dot(s, values[:, cols])


def mixed_kernel(query, inside, history, head_gain, normed):
    @functools.partial(by_tiles, query.shape[0])
    def _(rows):
        for h in range(2):
            cols = slice(h * HD, (h + 1) * HD)
            m = inside[rows, cols] + dot(query[rows, cols], history[h])
            scale = lax.rsqrt(jnp.mean(m * m, axis=-1, keepdims=True) + 1e-06)
            normed[rows, cols] = (m * scale * head_gain[:, cols]).astype(BF)


def prep_kernel(place, *refs):
    norm_gain, scaled_out, factor_out, scaled, factor, sems = refs[8:]
    length, width = scaled.shape

    @functools.partial(by_tiles, length)
    def _(rows):
        total = jnp.zeros((256, W), F32)
        for at, piece in pieces_of(place, refs[:4], refs[4:8]):
            v = piece[rows, :].astype(F32)
            total = total + v * v
            scaled[rows, pl.ds(at, W)] = (v * norm_gain[:, pl.ds(at, W)]).astype(BF)
        mean = jnp.sum(total, axis=-1, keepdims=True) / width
        factor[rows, :] = jnp.broadcast_to(lax.rsqrt(mean + 1e-05), (256, factor.shape[1]))

    copies = [
        pltpu.make_async_copy(scaled, scaled_out, sems.at[0]),
        pltpu.make_async_copy(factor, factor_out, sems.at[1]),
    ]
    for c in copies:
        c.start()
    for c in copies:
        c.wait()


def hidden_kernel(scaled_from, factor_from, weights, hidden, downs, x, factor, gate, up, sems):
    length, _ = x.shape
    ff = hidden.shape[1]

    def tile(s):
        at = pl.multiple_of(s * W, W)
        g = pltpu.make_async_copy(weights.at[:, pl.ds(at, W)], gate.at[s], sems.at[0, s])
        u = pltpu.make_async_copy(weights.at[:, pl.ds(ff + at, W)], up.at[s], sems.at[1, s])
        return g, u

    def rows_of(r):
        rows = pl.ds(r * W, W)
        return pltpu.make_async_copy(scaled_from.at[rows, :], x.at[rows, :], sems.at[2, r])

    scales = pltpu.make_async_copy(factor_from, factor, sems.at[2, 3])
    last = pltpu.make_async_copy(weights.at[:, 2 * ff : 3 * ff], downs, sems.at[3, 0])
    rows_of(0).start()
    for c in tile(0):
        c.start()
    scales.start()
    for r in range(1, length // W):
        rows_of(r).start()
    for s in range(1, ff // W):
        for c in tile(s):
            c.start()
    last.start()

    def step(s, _):
        for c in tile(s):
            c.wait()
        cols = pl.ds(pl.multiple_of(s * W, W), W)

        @pl.when(s == 0)
        def _():
            scales.wait()

        for r in range(length // W):

            @pl.when(s == 0)
            def _():
                rows_of(r).wait()

            rows = slice(r * W, (r + 1) * W)
            f = jnp.concatenate([factor[rows, :]] * (W // factor.shape[1]), axis=1)
            g = dot(x[rows, :], gate[s]) * f
            u = dot(x[rows, :], up[s]) * f
            hidden[rows, cols] = (g / (1.0 + jnp.exp(-g)) * u).astype(BF)
        return 0

    lax.fori_loop(0, ff // W, step, 0)
    last.wait()


def sum_at_owner(part, base):
    arrived = {}
    for d in (2, 1, 3, 0):
        core = lax.axis_index("core")
        give = part(d, 1 - core)
        got = swap(give)
        keep = part(d, core)
        both = keep.astype(F32) + got.astype(F32)
        if d == 0:
            both = base + both
        else:
            both = shift(both.astype(BF), "x", d).astype(F32)
        arrived[d] = both
    return arrived[0] + arrived[1] + arrived[2] + arrived[3]


def earlier_blocks(state, fillers):
    z, y = lax.axis_index("z"), lax.axis_index("y")
    other = lax.ppermute(state, "z", [(i, i ^ 1) for i in range(lax.axis_size("z"))]).astype(F32)
    row = state.astype(F32) + other
    before = jnp.where(z % 2 == 1, other, 0.0)
    pair = row.astype(BF)
    found = [shift(pair, "z", d) for d in (4, 2, 6)]
    filled = fillers()
    *found, filled = lax.optimization_barrier((*found, filled))
    for d, s in zip((4, 2, 6), found):
        s = s.astype(F32)
        row = row + s
        before = before + jnp.where(z >= d, s, 0.0)
    row = row.astype(BF)
    for d in (2, 1, 3):
        before = before + jnp.where(y >= d, shift(row, "y", d).astype(F32), 0.0)
    return before.astype(BF), filled


def body(tokens, w_query, w_key, w_value, head_gain, w_out, norm_gain, w_gate, w_up, w_down):
    length = tokens.shape[0]
    width = norm_gain.shape[0]
    heads = w_query.shape[1] // HD
    ff = w_gate.shape[1]
    place = jnp.stack([lax.axis_index(a) for a in ("x", "core")]).astype(jnp.int32)
    packed = jnp.concatenate([w_gate, w_up, w_down.T], axis=1)
    weights = lax.all_gather(packed, SEQ, axis=0, tiled=True)
    mine, theirs = spread(tokens)
    rows, row = (length, W), (length, width)
    whole, keys, values, state = kernel_of(
        keys_kernel,
        [(row, BF), (rows, BF), (rows, BF), ((heads, HD, HD), BF)],
        place,
        *mine,
        *theirs,
        (w_key,),
        (w_value,),
        scratch=[
            pltpu.VMEM((width, W), BF),
            pltpu.VMEM((width, W), BF),
            pltpu.SemaphoreType.DMA((2,)),
        ],
        flops=4 * length * width * W,
    )

    def query_of():
        return kernel_of(
            query_kernel, [(rows, BF)], whole, w_query, flops=2 * length * width * W
        )[0]

    history, query = earlier_blocks(state, query_of)
    (inside,) = kernel_of(
        inside_kernel, [(rows, F32)], query, keys, values, flops=4 * length * length * W
    )
    (normed,) = kernel_of(
        mixed_kernel,
        [(rows, BF)],
        query,
        inside,
        history,
        head_gain.reshape(1, W),
        flops=2 * length * HD * W,
    )
    x = lax.axis_index("x")

    def attn(d, c):
        at = (2 * lax.rem(x + d, 4) + c) * W
        return dot(normed, lax.dynamic_slice_in_dim(w_out, at, W, 1)).astype(BF)

    resid = sum_at_owner(attn, tokens)
    mine, theirs = spread(resid.astype(BF))
    n = ff // W
    scaled, factor = kernel_of(
        prep_kernel,
        [(row, BF, pltpu.HBM), ((length, HD), F32, pltpu.HBM)],
        place,
        *mine,
        *theirs,
        norm_gain.reshape(1, width),
        scratch=[
            pltpu.VMEM(row, BF),
            pltpu.VMEM((length, HD), F32),
            pltpu.SemaphoreType.DMA((2,)),
        ],
        flops=4 * length * width,
    )
    hidden, downs = kernel_of(
        hidden_kernel,
        [((length, ff), BF), ((width, ff), BF)],
        (scaled,),
        (factor,),
        (weights,),
        scratch=[
            pltpu.VMEM(row, BF),
            pltpu.VMEM((length, HD), F32),
            pltpu.VMEM((n, width, W), BF),
            pltpu.VMEM((n, width, W), BF),
            pltpu.SemaphoreType.DMA((4, 4)),
        ],
        flops=4 * length * width * ff,
        grant=20,
    )

    def mlp(d, c):
        at = (2 * lax.rem(x + d, 4) + c) * W
        w = lax.dynamic_slice_in_dim(downs, at, W, 0)
        return dot(hidden, w, ((1,), (1,))).astype(BF)

    return sum_at_owner(mlp, resid).astype(BF)


def solution(mesh):
    finer = Mesh(mesh.devices.reshape(4, 8, 4, 2), SEQ + TP)
    return jax.shard_map(
        body,
        mesh=finer,
        in_specs=(
            P(SEQ, TP),
            P(None, TP),
            P(None, TP),
            P(None, TP),
            P(TP),
            P(TP, None),
            P(),
            P(SEQ, TP),
            P(SEQ, TP),
            P(TP, SEQ),
        ),
        out_specs=P(SEQ, TP),
        check_vma=False,
    )
```

time: 356 us -> 181 us (0.51)
  waiting for transfers between devices: 246 us -> 78.2 us
  starting transfers between devices: 8.92 us -> 50.5 us
  blocking collectives: 30.5 us -> 0 us
  matrix products: 38.1 us -> 9.5 us
  Pallas kernels: 0 us -> 23.8 us
  other arithmetic: 12.2 us -> 2.15 us
    all_gather x3 -> x1, waiting for transfers between devices: 128 us -> 6.07 us  [body(): weights = lax.all_gather(packed, SEQ, axis=0, tiled=True)]
    psum x1 -> x0, waiting for transfers between devices: 79.1 us -> none  [body(): lax.psum(partial_value.astype(jnp.bfloat16), 'tp').astype(jnp.float32)]
    ppermute x0 -> x35, waiting for transfers between devices: none -> 72.1 us  [the longest x34 69.3 us: shift(): return lax.ppermute(a, axis, [(i, (i + by) % n) for i in range(n)])]
    ppermute x0 -> x35, starting transfers between devices: none -> 50.5 us  [the longest x34 48.9 us: shift(): return lax.ppermute(a, axis, [(i, (i + by) % n) for i in range(n)])]
    all_to_all x1 -> x0, waiting for transfers between devices: 37.6 us -> none  [sum_at_owner(): lax.all_to_all(tiles, axis, split_axis=0, concat_axis=0, tiled=True)]
    all_gather x2 -> x0, blocking collectives: 30.5 us -> none  [entering(): pieces = lax.all_gather(total.astype(jnp.bfloat16), axis)]
    dot_general x9 -> x16, matrix products: 38.1 us -> 9.5 us  [dot(): return lax.dot_general(a, b, (dims, ((), ())), preferred_element_type=F32)]
    pallas_call x0 -> x6, Pallas kernels: none -> 23.8 us  [kernel_of(): pl.pallas_call(body, in_specs=specs, out_specs=[stays if space else vmem...]
  transfers between devices with their start and end apart: 5 -> 36, of which waited for: 5 -> 18; matrix products, arithmetic and copies ran while one was open for 5% -> 4% of each run, Pallas kernels for 0% -> 7%
where the time goes in v1:
time: 181 us
  waiting for transfers between devices  78.2 us (43%)
  starting transfers between devices  50.5 us (28%)
  Pallas kernels  23.8 us (13%)
  between operations  13.7 us (8%)
  matrix products  9.5 us (5%)
  local copies, waits for them, and re-layouts  2.76 us (2%)
  other arithmetic  2.15 us (1%)
    ppermute x34, waiting for transfers between devices, shift(): return lax.ppermute(a, axis, [(i, (i + by) % n) for i in range(n)])  69.3 us
    ppermute x34, starting transfers between devices, shift(): return lax.ppermute(a, axis, [(i, (i + by) % n) for i in range(n)])  48.9 us
    pallas_call x6, Pallas kernels, kernel_of(): pl.pallas_call(body, in_specs=specs, out_specs=[stays if space else vmem...  23.8 us
    dot_general x16, matrix products, dot(): return lax.dot_general(a, b, (dims, ((), ())), preferred_element_type=F32)  9.5 us
    all_gather x1, waiting for transfers between devices, body(): weights = lax.all_gather(packed, SEQ, axis=0, tiled=True)  6.07 us
  transfers between devices with their start and end apart: 36, of which 18 were waited for; matrix products, arithmetic and copies ran while one was open for 4% of the time, Pallas kernels for 7%

profile of v1, /device:TPU:1, one launch (start us, length us, event | category | flops | bytes accessed | tf_op | source)
XLA Modules:
  0.0 180.6 jit_solution(8385907688499149901)
XLA Ops:
  6.5 1.9 %pad_maximum_fusion = bf16[64,3072]{1,0:T(8,128)(2,1)} fusion(bf16[64,1024]{1,0:T(8,128)(2,1)} %bitcast.23, bf16[64,1024]{1,0:T(8,128)(2,1)} %param.18, bf16[64,1024]{1,0:T(8,128)(2,1)} %param.17), kind=kLoop, calls=%fused_computation.55 | loop fusion | flops 1179648 | bytes 786432 | tf_op jit(solution)/shard_map/concatenate | solution.py:261
  8.5 3.4 %collective-permute-start.2 = (bf16[768,256]{1,0:T(8,128)(2,1)}, bf16[768,256]{1,0:T(8,128)(2,1)S(1)}, u32[]{:S(2)}, u32[]{:S(2)}) collective-permute-start(bf16[768,256]{1,0:T(8,128)(2,1)} %refs_0_.1), channel_id=1, source_target_pairs={{0,6},{2,0},{4,2},{6,4},{1,7},{3,1},{5,3},{7,5},{8,14},{10,8},{12,... | collective-permute-start | bytes 1179656 | tf_op jit(solution)/shard_map/ppermute | solution.py:22
  13.0 1.5 collective-permute-start.3
  14.5 8.4 %collective-permute-done.2.refs_3_ = bf16[768,256]{1,0:T(8,128)(2,1)S(1)} collective-permute-done((bf16[768,256]{1,0:T(8,128)(2,1)}, bf16[768,256]{1,0:T(8,128)(2,1)S(1)}, u32[]{:S(2)}, u32[]{:S(2)}) %collective-permute-start.2) | collective-permute-done | bytes 393248 | tf_op jit(solution)/shard_map/ppermute | solution.py:22
  22.9 7.0 %collective-permute-start.6 = (bf16[768,256]{1,0:T(8,128)(2,1)S(1)}, bf16[768,256]{1,0:T(8,128)(2,1)S(1)}, u32[]{:S(2)}, u32[]{:S(2)}) collective-permute-start(bf16[768,256]{1,0:T(8,128)(2,1)S(1)} %collective-permute-done.2.refs_3_), channel_id=1, source_target_pairs={{0,1},{1,0},{2,3},{3,2},{4,5},{5,4},{6,7},{7,6},{8,9},{9,8},{10,11... | collective-permute-start | bytes 1179656 | tf_op jit(solution)/shard_map/ppermute | solution.py:22
  29.9 3.2 %collective-permute-done.refs_1_ = bf16[768,256]{1,0:T(8,128)(2,1)S(1)} collective-permute-done((bf16[768,256]{1,0:T(8,128)(2,1)}, bf16[768,256]{1,0:T(8,128)(2,1)S(1)}, u32[]{:S(2)}, u32[]{:S(2)}) %collective-permute-start) | collective-permute-done | bytes 393248 | tf_op jit(solution)/shard_map/ppermute | solution.py:22
  33.6 1.4 collective-permute-done.4.refs_5_
  36.0 5.0 %shard_map.100 = (bf16[768,2048]{1,0:T(8,128)(2,1)S(1)}, bf16[768,256]{1,0:T(8,128)(2,1)S(1)}, bf16[768,256]{1,0:T(8,128)(2,1)S(1)}, bf16[2,128,128]{2,1,0:T(8,128)(2,1)S(1)}) custom-call(s32[2]{0:T(128)S(1)} %pad_add_fusion.place, bf16[768,256]{1,0:T(8,128)(2,1)S(1)} %copy-done.2, bf16[768,256]{1,0:T(8,128)(2,1)S(1)} %collective-permute-done.refs_1_, ...), custom_call_target="tpu_custom_call" | custom-call | flops 1610612736 | bytes 8388608 | tf_op jit(solution)/shard_map/pallas_call | solution.py:57
  41.8 1.7 collective-permute-start.7
  43.4 2.9 %collective-permute-done.7 = bf16[2,128,128]{2,1,0:T(8,128)(2,1)S(1)} collective-permute-done((bf16[2,128,128]{2,1,0:T(8,128)(2,1)S(1)}, bf16[2,128,128]{2,1,0:T(8,128)(2,1)S(1)}, u32[]{:S(2)}, u32[]{:S(2)}) %collective-permute-start.7) | collective-permute-done | bytes 65568 | tf_op jit(solution)/shard_map/ppermute | solution.py:238
  46.3 6.2 %collective-permute-start.10 = (bf16[2,128,128]{2,1,0:T(8,128)(2,1)S(1)}, bf16[2,128,128]{2,1,0:T(8,128)(2,1)S(1)}, u32[]{:S(2)}, u32[]{:S(2)}) collective-permute-start(bf16[2,128,128]{2,1,0:T(8,128)(2,1)S(1)} %fusion.55), channel_id=1, source_target_pairs={{0,48},{8,56},{16,0},{24,8},{32,16},{40,24},{48,32},{56,40},{1,49}... | collective-permute-start | bytes 196616 | tf_op jit(solution)/shard_map/ppermute | solution.py:22
  52.5 4.0 %collective-permute-start.8 = (bf16[2,128,128]{2,1,0:T(8,128)(2,1)S(1)}, bf16[2,128,128]{2,1,0:T(8,128)(2,1)S(1)}, u32[]{:S(2)}, u32[]{:S(2)}) collective-permute-start(bf16[2,128,128]{2,1,0:T(8,128)(2,1)S(1)} %fusion.55), channel_id=1, source_target_pairs={{0,32},{8,40},{16,48},{24,56},{32,0},{40,8},{48,16},{56,24},{1,33}... | collective-permute-start | bytes 196616 | tf_op jit(solution)/shard_map/ppermute | solution.py:22
  58.1 2.7 %collective-permute-done.8 = bf16[2,128,128]{2,1,0:T(8,128)(2,1)S(1)} collective-permute-done((bf16[2,128,128]{2,1,0:T(8,128)(2,1)S(1)}, bf16[2,128,128]{2,1,0:T(8,128)(2,1)S(1)}, u32[]{:S(2)}, u32[]{:S(2)}) %collective-permute-start.8) | collective-permute-done | bytes 65568 | tf_op jit(solution)/shard_map/ppermute | solution.py:22
  60.9 2.9 %collective-permute-start.13 = (bf16[2,128,128]{2,1,0:T(8,128)(2,1)S(1)}, bf16[2,128,128]{2,1,0:T(8,128)(2,1)S(1)}, u32[]{:S(2)}, u32[]{:S(2)}) collective-permute-start(bf16[2,128,128]{2,1,0:T(8,128)(2,1)S(1)} %fusion.46), channel_id=1, source_target_pairs={{0,192},{64,0},{128,64},{192,128},{1,193},{65,1},{129,65},{193,129... | collective-permute-start | bytes 196616 | tf_op jit(solution)/shard_map/ppermute | solution.py:22
  63.8 1.9 %collective-permute-start.11 = (bf16[2,128,128]{2,1,0:T(8,128)(2,1)S(1)}, bf16[2,128,128]{2,1,0:T(8,128)(2,1)S(1)}, u32[]{:S(2)}, u32[]{:S(2)}) collective-permute-start(bf16[2,128,128]{2,1,0:T(8,128)(2,1)S(1)} %fusion.46), channel_id=1, source_target_pairs={{0,128},{64,192},{128,0},{192,64},{1,129},{65,193},{129,1},{193,65... | collective-permute-start | bytes 196616 | tf_op jit(solution)/shard_map/ppermute | solution.py:22
  66.7 1.9 %shard_map.102.inside = f32[768,256]{1,0:T(8,128)S(1)} custom-call(bf16[768,256]{1,0:T(8,128)(2,1)S(1)} %shard_map.101.query, bf16[768,256]{1,0:T(8,128)(2,1)S(1)} %copy-done.7, bf16[768,256]{1,0:T(8,128)(2,1)S(1)} %copy-done.9), custom_call_target="tpu_custom_call" | custom-call | flops 603979776 | bytes 8388608 | tf_op jit(solution)/shard_map/pallas_call | solution.py:57
  70.1 4.1 %collective-permute-start.14 = (bf16[768,256]{1,0:T(8,128)(2,1)S(1)}, bf16[768,256]{1,0:T(8,128)(2,1)}, u32[]{:S(2)}, u32[]{:S(2)}) collective-permute-start(bf16[768,256]{1,0:T(8,128)(2,1)S(1)} %convolution_convert_fusion.14), channel_id=1, source_target_pairs={{0,1},{1,0},{2,3},{3,2},{4,5},{5,4},{6,7},{7,6},{8,9},{9,8},{10,11... | collective-permute-start | bytes 1179656 | tf_op jit(solution)/shard_map/ppermute | solution.py:22
  77.2 1.3 collective-permute-start.18
  80.2 16.8 %collective-permute-done.16 = bf16[768,256]{1,0:T(8,128)(2,1)} collective-permute-done((bf16[768,256]{1,0:T(8,128)(2,1)S(1)}, bf16[768,256]{1,0:T(8,128)(2,1)}, u32[]{:S(2)}, u32[]{:S(2)}) %collective-permute-start.16) | collective-permute-done | bytes 393248 | tf_op jit(solution)/shard_map/ppermute | solution.py:22
  97.7 1.8 %fusion.72 = (bf16[768,256]{1,0:T(8,128)(2,1)S(1)}, f32[768,256]{1,0:T(8,128)S(1)}) fusion(bf16[768,256]{1,0:T(8,128)(2,1)} %collective-permute-done.20, bf16[768,256]{1,0:T(8,128)(2,1)} %collective-permute-done.18, bf16[768,256]{1,0:T(8,128)(2,1)} %collective-permute-done.16, bf16[768,256]{1,0:T(8,128)(2,1)} %collective-permute-done.14, ...), kind=kOutput, calls=%fused_computation.98 | convolution fusion | flops 103219200 | bytes 3670020 | tf_op jit(solution)/shard_map/dot_general | solution.py:69
  99.5 3.3 %collective-permute-start.23 = (bf16[768,256]{1,0:T(8,128)(2,1)S(1)}, bf16[768,256]{1,0:T(8,128)(2,1)S(1)}, u32[]{:S(2)}, u32[]{:S(2)}) collective-permute-start(bf16[768,256]{1,0:T(8,128)(2,1)S(1)} %get-tuple-element.29.refs_0_), channel_id=1, source_target_pairs={{0,6},{2,0},{4,2},{6,4},{1,7},{3,1},{5,3},{7,5},{8,14},{10,8},{12,... | collective-permute-start | bytes 1179656 | tf_op jit(solution)/shard_map/ppermute | solution.py:22
  104.5 14.5 %collective-permute-done.23.refs_3_ = bf16[768,256]{1,0:T(8,128)(2,1)S(1)} collective-permute-done((bf16[768,256]{1,0:T(8,128)(2,1)S(1)}, bf16[768,256]{1,0:T(8,128)(2,1)S(1)}, u32[]{:S(2)}, u32[]{:S(2)}) %collective-permute-start.23) | collective-permute-done | bytes 393248 | tf_op jit(solution)/shard_map/ppermute | solution.py:22
  119.0 1.5 collective-permute-start.27
  120.5 2.7 %collective-permute-done.21.refs_1_ = bf16[768,256]{1,0:T(8,128)(2,1)S(1)} collective-permute-done((bf16[768,256]{1,0:T(8,128)(2,1)S(1)}, bf16[768,256]{1,0:T(8,128)(2,1)S(1)}, u32[]{:S(2)}, u32[]{:S(2)}) %collective-permute-start.21) | collective-permute-done | bytes 393248 | tf_op jit(solution)/shard_map/ppermute | solution.py:22
  124.0 1.3 collective-permute-done.25.refs_5_
  125.3 3.7 %shard_map.104 = (bf16[768,2048]{1,0:T(8,128)(2,1)}, f32[768,128]{1,0:T(8,128)}) custom-call(s32[2]{0:T(128)S(1)} %pad_add_fusion.place, bf16[768,256]{1,0:T(8,128)(2,1)S(1)} %get-tuple-element.29.refs_0_, bf16[768,256]{1,0:T(8,128)(2,1)S(1)} %collective-permute-done.21.refs_1_, bf16[768,256]{1,0:T(8,128)(2,1)S(1)} %collective-permute-done.22.refs_2_, ...), custom_call_target="tpu_custom_call" | custom-call | flops 6291456 | bytes 8388608 | tf_op jit(solution)/shard_map/pallas_call | solution.py:57
  129.0 6.1 %all-gather.2.cloned.1.call-done.weights = bf16[2048,3072]{1,0:T(8,128)(2,1)} async-done(((bf16[64,3072]{1,0:T(8,128)(2,1)}), bf16[2048,3072]{1,0:T(8,128)(2,1)}) %all-gather.2.cloned.1.call-update) | async-done | bytes 12582928 | tf_op jit(solution)/shard_map/all_gather | solution.py:262
  135.1 11.0 %shard_map.105 = (bf16[768,1024]{1,0:T(8,128)(2,1)S(1)}, bf16[2048,1024]{1,0:T(8,128)(2,1)S(1)}) custom-call(bf16[768,2048]{1,0:T(8,128)(2,1)} %get-tuple-element.25.scaled_from, f32[768,128]{1,0:T(8,128)} %get-tuple-element.26.factor_from, bf16[2048,3072]{1,0:T(8,128)(2,1)} %all-gather.2.cloned.1.call-done.weights), custom_call_target="tpu_custom_call" | custom-call | flops 6442450944 | bytes 8388608 | tf_op jit(solution)/shard_map/pallas_call | solution.py:57
  152.0 2.6 %collective-permute-start.32 = (bf16[768,256]{1,0:T(8,128)(2,1)S(1)}, bf16[768,256]{1,0:T(8,128)(2,1)S(1)}, u32[]{:S(2)}, u32[]{:S(2)}) collective-permute-start(bf16[768,256]{1,0:T(8,128)(2,1)S(1)} %fusion.5), channel_id=1, source_target_pairs={{0,4},{2,6},{4,0},{6,2},{1,5},{3,7},{5,1},{7,3},{8,12},{10,14},{12... | collective-permute-start | bytes 1179656 | tf_op jit(solution)/shard_map/ppermute | solution.py:22
  156.0 7.0 %collective-permute-done.30 = bf16[768,256]{1,0:T(8,128)(2,1)S(1)} collective-permute-done((bf16[768,256]{1,0:T(8,128)(2,1)S(1)}, bf16[768,256]{1,0:T(8,128)(2,1)S(1)}, u32[]{:S(2)}, u32[]{:S(2)}) %collective-permute-start.30) | collective-permute-done | bytes 393248 | tf_op jit(solution)/shard_map/ppermute | solution.py:22
  163.0 8.1 %collective-permute-done.32 = bf16[768,256]{1,0:T(8,128)(2,1)S(1)} collective-permute-done((bf16[768,256]{1,0:T(8,128)(2,1)S(1)}, bf16[768,256]{1,0:T(8,128)(2,1)S(1)}, u32[]{:S(2)}, u32[]{:S(2)}) %collective-permute-start.32) | collective-permute-done | bytes 393248 | tf_op jit(solution)/shard_map/ppermute | solution.py:22
  172.3 1.5 fusion.15
  (88 shorter events, 23.5 us)
Async XLA Ops:
  6.5 128.5 %all-gather.2.cloned.1.call-start = ((), (), s32[]{:S(2)}) async-start(), calls=%async_computation | async-start | bytes 12976128 | tf_op jit(solution)/shard_map/all_gather | solution.py:262
  8.5 14.4 %collective-permute-start.2 = (bf16[768,256]{1,0:T(8,128)(2,1)}, bf16[768,256]{1,0:T(8,128)(2,1)S(1)}, u32[]{:S(2)}, u32[]{:S(2)}) collective-permute-start(bf16[768,256]{1,0:T(8,128)(2,1)} %refs_0_.1), channel_id=1, source_target_pairs={{0,6},{2,0},{4,2},{6,4},{1,7},{3,1},{5,3},{7,5},{8,14},{10,8},{12,... | collective-permute-start | bytes 1179656 | tf_op jit(solution)/shard_map/ppermute | solution.py:22
  11.8 18.1 %collective-permute-start.1 = (bf16[768,256]{1,0:T(8,128)(2,1)}, bf16[768,256]{1,0:T(8,128)(2,1)S(1)}, u32[]{:S(2)}, u32[]{:S(2)}) collective-permute-start(bf16[768,256]{1,0:T(8,128)(2,1)} %refs_0_.1), channel_id=1, source_target_pairs={{0,4},{2,6},{4,0},{6,2},{1,5},{3,7},{5,1},{7,3},{8,12},{10,14},{12... | collective-permute-start | bytes 1179656 | tf_op jit(solution)/shard_map/ppermute | solution.py:22
  12.4 20.8 %collective-permute-start = (bf16[768,256]{1,0:T(8,128)(2,1)}, bf16[768,256]{1,0:T(8,128)(2,1)S(1)}, u32[]{:S(2)}, u32[]{:S(2)}) collective-permute-start(bf16[768,256]{1,0:T(8,128)(2,1)} %refs_0_.1), channel_id=1, source_target_pairs={{0,2},{2,4},{4,6},{6,0},{1,3},{3,5},{5,7},{7,1},{8,10},{10,12},{12... | collective-permute-start | bytes 1179656 | tf_op jit(solution)/shard_map/ppermute | solution.py:22
  13.0 20.6 %collective-permute-start.3 = (bf16[768,256]{1,0:T(8,128)(2,1)}, bf16[768,256]{1,0:T(8,128)(2,1)S(1)}, u32[]{:S(2)}, u32[]{:S(2)}) collective-permute-start(bf16[768,256]{1,0:T(8,128)(2,1)} %refs_0_.1), channel_id=1, source_target_pairs={{0,1},{1,0},{2,3},{3,2},{4,5},{5,4},{6,7},{7,6},{8,9},{9,8},{10,11... | collective-permute-start | bytes 1179656 | tf_op jit(solution)/shard_map/ppermute | solution.py:22
  22.9 10.7 %collective-permute-start.6 = (bf16[768,256]{1,0:T(8,128)(2,1)S(1)}, bf16[768,256]{1,0:T(8,128)(2,1)S(1)}, u32[]{:S(2)}, u32[]{:S(2)}) collective-permute-start(bf16[768,256]{1,0:T(8,128)(2,1)S(1)} %collective-permute-done.2.refs_3_), channel_id=1, source_target_pairs={{0,1},{1,0},{2,3},{3,2},{4,5},{5,4},{6,7},{7,6},{8,9},{9,8},{10,11... | collective-permute-start | bytes 1179656 | tf_op jit(solution)/shard_map/ppermute | solution.py:22
  29.9 3.7 %collective-permute-start.5 = (bf16[768,256]{1,0:T(8,128)(2,1)S(1)}, bf16[768,256]{1,0:T(8,128)(2,1)S(1)}, u32[]{:S(2)}, u32[]{:S(2)}) collective-permute-start(bf16[768,256]{1,0:T(8,128)(2,1)S(1)} %collective-permute-done.1.refs_2_), channel_id=1, source_target_pairs={{0,1},{1,0},{2,3},{3,2},{4,5},{5,4},{6,7},{7,6},{8,9},{9,8},{10,11... | collective-permute-start | bytes 1179656 | tf_op jit(solution)/shard_map/ppermute | solution.py:22
  41.8 4.5 %collective-permute-start.7 = (bf16[2,128,128]{2,1,0:T(8,128)(2,1)S(1)}, bf16[2,128,128]{2,1,0:T(8,128)(2,1)S(1)}, u32[]{:S(2)}, u32[]{:S(2)}) collective-permute-start(bf16[2,128,128]{2,1,0:T(8,128)(2,1)S(1)} %get-tuple-element.17), channel_id=1, source_target_pairs={{0,8},{8,0},{16,24},{24,16},{32,40},{40,32},{48,56},{56,48},{1,9},... | collective-permute-start | bytes 196616 | tf_op jit(solution)/shard_map/ppermute | solution.py:238
  46.3 11.6 %collective-permute-start.10 = (bf16[2,128,128]{2,1,0:T(8,128)(2,1)S(1)}, bf16[2,128,128]{2,1,0:T(8,128)(2,1)S(1)}, u32[]{:S(2)}, u32[]{:S(2)}) collective-permute-start(bf16[2,128,128]{2,1,0:T(8,128)(2,1)S(1)} %fusion.55), channel_id=1, source_target_pairs={{0,48},{8,56},{16,0},{24,8},{32,16},{40,24},{48,32},{56,40},{1,49}... | collective-permute-start | bytes 196616 | tf_op jit(solution)/shard_map/ppermute | solution.py:22
  52.5 5.6 %collective-permute-start.9 = (bf16[2,128,128]{2,1,0:T(8,128)(2,1)S(1)}, bf16[2,128,128]{2,1,0:T(8,128)(2,1)S(1)}, u32[]{:S(2)}, u32[]{:S(2)}) collective-permute-start(bf16[2,128,128]{2,1,0:T(8,128)(2,1)S(1)} %fusion.55), channel_id=1, source_target_pairs={{0,16},{8,24},{16,32},{24,40},{32,48},{40,56},{48,0},{56,8},{1,17}... | collective-permute-start | bytes 196616 | tf_op jit(solution)/shard_map/ppermute | solution.py:22
  52.5 8.3 %collective-permute-start.8 = (bf16[2,128,128]{2,1,0:T(8,128)(2,1)S(1)}, bf16[2,128,128]{2,1,0:T(8,128)(2,1)S(1)}, u32[]{:S(2)}, u32[]{:S(2)}) collective-permute-start(bf16[2,128,128]{2,1,0:T(8,128)(2,1)S(1)} %fusion.55), channel_id=1, source_target_pairs={{0,32},{8,40},{16,48},{24,56},{32,0},{40,8},{48,16},{56,24},{1,33}... | collective-permute-start | bytes 196616 | tf_op jit(solution)/shard_map/ppermute | solution.py:22
  60.9 7.7 %collective-permute-start.13 = (bf16[2,128,128]{2,1,0:T(8,128)(2,1)S(1)}, bf16[2,128,128]{2,1,0:T(8,128)(2,1)S(1)}, u32[]{:S(2)}, u32[]{:S(2)}) collective-permute-start(bf16[2,128,128]{2,1,0:T(8,128)(2,1)S(1)} %fusion.46), channel_id=1, source_target_pairs={{0,192},{64,0},{128,64},{192,128},{1,193},{65,1},{129,65},{193,129... | collective-permute-start | bytes 196616 | tf_op jit(solution)/shard_map/ppermute | solution.py:22
  63.8 5.0 %collective-permute-start.12 = (bf16[2,128,128]{2,1,0:T(8,128)(2,1)S(1)}, bf16[2,128,128]{2,1,0:T(8,128)(2,1)S(1)}, u32[]{:S(2)}, u32[]{:S(2)}) collective-permute-start(bf16[2,128,128]{2,1,0:T(8,128)(2,1)S(1)} %fusion.46), channel_id=1, source_target_pairs={{0,64},{64,128},{128,192},{192,0},{1,65},{65,129},{129,193},{193,1... | collective-permute-start | bytes 196616 | tf_op jit(solution)/shard_map/ppermute | solution.py:22
  63.8 5.0 %collective-permute-start.11 = (bf16[2,128,128]{2,1,0:T(8,128)(2,1)S(1)}, bf16[2,128,128]{2,1,0:T(8,128)(2,1)S(1)}, u32[]{:S(2)}, u32[]{:S(2)}) collective-permute-start(bf16[2,128,128]{2,1,0:T(8,128)(2,1)S(1)} %fusion.46), channel_id=1, source_target_pairs={{0,128},{64,192},{128,0},{192,64},{1,129},{65,193},{129,1},{193,65... | collective-permute-start | bytes 196616 | tf_op jit(solution)/shard_map/ppermute | solution.py:22
  70.1 10.0 %collective-permute-start.14 = (bf16[768,256]{1,0:T(8,128)(2,1)S(1)}, bf16[768,256]{1,0:T(8,128)(2,1)}, u32[]{:S(2)}, u32[]{:S(2)}) collective-permute-start(bf16[768,256]{1,0:T(8,128)(2,1)S(1)} %convolution_convert_fusion.14), channel_id=1, source_target_pairs={{0,1},{1,0},{2,3},{3,2},{4,5},{5,4},{6,7},{7,6},{8,9},{9,8},{10,11... | collective-permute-start | bytes 1179656 | tf_op jit(solution)/shard_map/ppermute | solution.py:22
  75.8 2.8 %collective-permute-start.19 = (bf16[768,256]{1,0:T(8,128)(2,1)S(1)}, bf16[768,256]{1,0:T(8,128)(2,1)S(1)}, u32[]{:S(2)}, u32[]{:S(2)}) collective-permute-start(bf16[768,256]{1,0:T(8,128)(2,1)S(1)} %convolution_convert_fusion.8), channel_id=1, source_target_pairs={{0,1},{1,0},{2,3},{3,2},{4,5},{5,4},{6,7},{7,6},{8,9},{9,8},{10,11... | collective-permute-start | bytes 1179656 | tf_op jit(solution)/shard_map/ppermute | solution.py:22
  76.7 20.3 %collective-permute-start.16 = (bf16[768,256]{1,0:T(8,128)(2,1)S(1)}, bf16[768,256]{1,0:T(8,128)(2,1)}, u32[]{:S(2)}, u32[]{:S(2)}) collective-permute-start(bf16[768,256]{1,0:T(8,128)(2,1)S(1)} %fusion.24), channel_id=1, source_target_pairs={{0,2},{2,4},{4,6},{6,0},{1,3},{3,5},{5,7},{7,1},{8,10},{10,12},{12... | collective-permute-start | bytes 1179656 | tf_op jit(solution)/shard_map/ppermute | solution.py:22
  77.2 19.8 %collective-permute-start.18 = (bf16[768,256]{1,0:T(8,128)(2,1)S(1)}, bf16[768,256]{1,0:T(8,128)(2,1)}, u32[]{:S(2)}, u32[]{:S(2)}) collective-permute-start(bf16[768,256]{1,0:T(8,128)(2,1)S(1)} %fusion.21), channel_id=1, source_target_pairs={{0,4},{2,6},{4,0},{6,2},{1,5},{3,7},{5,1},{7,3},{8,12},{10,14},{12... | collective-permute-start | bytes 1179656 | tf_op jit(solution)/shard_map/ppermute | solution.py:22
  78.8 18.9 %collective-permute-start.20 = (bf16[768,256]{1,0:T(8,128)(2,1)S(1)}, bf16[768,256]{1,0:T(8,128)(2,1)}, u32[]{:S(2)}, u32[]{:S(2)}) collective-permute-start(bf16[768,256]{1,0:T(8,128)(2,1)S(1)} %fusion.18), channel_id=1, source_target_pairs={{0,6},{2,0},{4,2},{6,4},{1,7},{3,1},{5,3},{7,5},{8,14},{10,8},{12,... | collective-permute-start | bytes 1179656 | tf_op jit(solution)/shard_map/ppermute | solution.py:22
  99.5 19.5 %collective-permute-start.23 = (bf16[768,256]{1,0:T(8,128)(2,1)S(1)}, bf16[768,256]{1,0:T(8,128)(2,1)S(1)}, u32[]{:S(2)}, u32[]{:S(2)}) collective-permute-start(bf16[768,256]{1,0:T(8,128)(2,1)S(1)} %get-tuple-element.29.refs_0_), channel_id=1, source_target_pairs={{0,6},{2,0},{4,2},{6,4},{1,7},{3,1},{5,3},{7,5},{8,14},{10,8},{12,... | collective-permute-start | bytes 1179656 | tf_op jit(solution)/shard_map/ppermute | solution.py:22
  102.8 17.8 %collective-permute-start.22 = (bf16[768,256]{1,0:T(8,128)(2,1)S(1)}, bf16[768,256]{1,0:T(8,128)(2,1)S(1)}, u32[]{:S(2)}, u32[]{:S(2)}) collective-permute-start(bf16[768,256]{1,0:T(8,128)(2,1)S(1)} %get-tuple-element.29.refs_0_), channel_id=1, source_target_pairs={{0,4},{2,6},{4,0},{6,2},{1,5},{3,7},{5,1},{7,3},{8,12},{10,14},{12... | collective-permute-start | bytes 1179656 | tf_op jit(solution)/shard_map/ppermute | solution.py:22
  102.8 20.5 %collective-permute-start.21 = (bf16[768,256]{1,0:T(8,128)(2,1)S(1)}, bf16[768,256]{1,0:T(8,128)(2,1)S(1)}, u32[]{:S(2)}, u32[]{:S(2)}) collective-permute-start(bf16[768,256]{1,0:T(8,128)(2,1)S(1)} %get-tuple-element.29.refs_0_), channel_id=1, source_target_pairs={{0,2},{2,4},{4,6},{6,0},{1,3},{3,5},{5,7},{7,1},{8,10},{10,12},{12... | collective-permute-start | bytes 1179656 | tf_op jit(solution)/shard_map/ppermute | solution.py:22
  103.5 20.5 %collective-permute-start.24 = (bf16[768,256]{1,0:T(8,128)(2,1)S(1)}, bf16[768,256]{1,0:T(8,128)(2,1)S(1)}, u32[]{:S(2)}, u32[]{:S(2)}) collective-permute-start(bf16[768,256]{1,0:T(8,128)(2,1)S(1)} %get-tuple-element.29.refs_0_), channel_id=1, source_target_pairs={{0,1},{1,0},{2,3},{3,2},{4,5},{5,4},{6,7},{7,6},{8,9},{9,8},{10,11... | collective-permute-start | bytes 1179656 | tf_op jit(solution)/shard_map/ppermute | solution.py:22
  119.0 4.9 %collective-permute-start.27 = (bf16[768,256]{1,0:T(8,128)(2,1)S(1)}, bf16[768,256]{1,0:T(8,128)(2,1)S(1)}, u32[]{:S(2)}, u32[]{:S(2)}) collective-permute-start(bf16[768,256]{1,0:T(8,128)(2,1)S(1)} %collective-permute-done.23.refs_3_), channel_id=1, source_target_pairs={{0,1},{1,0},{2,3},{3,2},{4,5},{5,4},{6,7},{7,6},{8,9},{9,8},{10,11... | collective-permute-start | bytes 1179656 | tf_op jit(solution)/shard_map/ppermute | solution.py:22
  120.5 3.4 %collective-permute-start.26 = (bf16[768,256]{1,0:T(8,128)(2,1)S(1)}, bf16[768,256]{1,0:T(8,128)(2,1)S(1)}, u32[]{:S(2)}, u32[]{:S(2)}) collective-permute-start(bf16[768,256]{1,0:T(8,128)(2,1)S(1)} %collective-permute-done.22.refs_2_), channel_id=1, source_target_pairs={{0,1},{1,0},{2,3},{3,2},{4,5},{5,4},{6,7},{7,6},{8,9},{9,8},{10,11... | collective-permute-start | bytes 1179656 | tf_op jit(solution)/shard_map/ppermute | solution.py:22
  147.3 3.3 %collective-permute-start.29 = (bf16[768,256]{1,0:T(8,128)(2,1)S(1)}, bf16[768,256]{1,0:T(8,128)(2,1)S(1)}, u32[]{:S(2)}, u32[]{:S(2)}) collective-permute-start(bf16[768,256]{1,0:T(8,128)(2,1)S(1)} %convolution_convert_fusion.4), channel_id=1, source_target_pairs={{0,1},{1,0},{2,3},{3,2},{4,5},{5,4},{6,7},{7,6},{8,9},{9,8},{10,11... | collective-permute-start | bytes 1179656 | tf_op jit(solution)/shard_map/ppermute | solution.py:22
  149.2 2.1 %collective-permute-start.31 = (bf16[768,256]{1,0:T(8,128)(2,1)S(1)}, bf16[768,256]{1,0:T(8,128)(2,1)S(1)}, u32[]{:S(2)}, u32[]{:S(2)}) collective-permute-start(bf16[768,256]{1,0:T(8,128)(2,1)S(1)} %convolution_convert_fusion.2), channel_id=1, source_target_pairs={{0,1},{1,0},{2,3},{3,2},{4,5},{5,4},{6,7},{7,6},{8,9},{9,8},{10,11... | collective-permute-start | bytes 1179656 | tf_op jit(solution)/shard_map/ppermute | solution.py:22
  150.0 6.0 %collective-permute-start.28 = (bf16[768,256]{1,0:T(8,128)(2,1)S(1)}, bf16[768,256]{1,0:T(8,128)(2,1)S(1)}, u32[]{:S(2)}, u32[]{:S(2)}) collective-permute-start(bf16[768,256]{1,0:T(8,128)(2,1)S(1)} %convolution_convert_fusion.6), channel_id=1, source_target_pairs={{0,1},{1,0},{2,3},{3,2},{4,5},{5,4},{6,7},{7,6},{8,9},{9,8},{10,11... | collective-permute-start | bytes 1179656 | tf_op jit(solution)/shard_map/ppermute | solution.py:22
  150.5 4.0 %collective-permute-start.33 = (bf16[768,256]{1,0:T(8,128)(2,1)S(1)}, bf16[768,256]{1,0:T(8,128)(2,1)S(1)}, u32[]{:S(2)}, u32[]{:S(2)}) collective-permute-start(bf16[768,256]{1,0:T(8,128)(2,1)S(1)} %convolution_convert_fusion), channel_id=1, source_target_pairs={{0,1},{1,0},{2,3},{3,2},{4,5},{5,4},{6,7},{7,6},{8,9},{9,8},{10,11... | collective-permute-start | bytes 1179656 | tf_op jit(solution)/shard_map/ppermute | solution.py:22
  151.3 11.7 %collective-permute-start.30 = (bf16[768,256]{1,0:T(8,128)(2,1)S(1)}, bf16[768,256]{1,0:T(8,128)(2,1)S(1)}, u32[]{:S(2)}, u32[]{:S(2)}) collective-permute-start(bf16[768,256]{1,0:T(8,128)(2,1)S(1)} %fusion.8), channel_id=1, source_target_pairs={{0,2},{2,4},{4,6},{6,0},{1,3},{3,5},{5,7},{7,1},{8,10},{10,12},{12... | collective-permute-start | bytes 1179656 | tf_op jit(solution)/shard_map/ppermute | solution.py:22
  152.0 19.1 %collective-permute-start.32 = (bf16[768,256]{1,0:T(8,128)(2,1)S(1)}, bf16[768,256]{1,0:T(8,128)(2,1)S(1)}, u32[]{:S(2)}, u32[]{:S(2)}) collective-permute-start(bf16[768,256]{1,0:T(8,128)(2,1)S(1)} %fusion.5), channel_id=1, source_target_pairs={{0,4},{2,6},{4,0},{6,2},{1,5},{3,7},{5,1},{7,3},{8,12},{10,14},{12... | collective-permute-start | bytes 1179656 | tf_op jit(solution)/shard_map/ppermute | solution.py:22
  155.2 17.1 %collective-permute-start.34 = (bf16[768,256]{1,0:T(8,128)(2,1)S(1)}, bf16[768,256]{1,0:T(8,128)(2,1)S(1)}, u32[]{:S(2)}, u32[]{:S(2)}) collective-permute-start(bf16[768,256]{1,0:T(8,128)(2,1)S(1)} %fusion.2), channel_id=1, source_target_pairs={{0,6},{2,0},{4,2},{6,4},{1,7},{3,1},{5,3},{7,5},{8,14},{10,8},{12,... | collective-permute-start | bytes 1179656 | tf_op jit(solution)/shard_map/ppermute | solution.py:22
  (14 other events, 199.2 us)
Sparse Core Ops, SparseCore 0:
  9.9 125.0 all-gather.1

commit v2 on v1

--- a/solution.py
+++ b/solution.py
@@ -191,21 +191,16 @@
             c.start()
     last.start()
 
+    scales.wait()
+    for r in range(length // W):
+        rows_of(r).wait()
+
     def step(s, _):
         for c in tile(s):
             c.wait()
         cols = pl.ds(pl.multiple_of(s * W, W), W)
 
-        @pl.when(s == 0)
-        def _():
-            scales.wait()
-
         for r in range(length // W):
-
-            @pl.when(s == 0)
-            def _():
-                rows_of(r).wait()
-
             rows = slice(r * W, (r + 1) * W)
             f = jnp.concatenate([factor[rows, :]] * (W // factor.shape[1]), axis=1)
             g = dot(x[rows, :], gate[s]) * f
@@ -217,20 +212,41 @@
     last.wait()
 
 
-def sum_at_owner(part, base):
-    arrived = {}
-    for d in (2, 1, 3, 0):
-        core = lax.axis_index("core")
+def halves_of(part):
+    core = lax.axis_index("core")
+
+    def both(d):
         give = part(d, 1 - core)
         got = swap(give)
-        keep = part(d, core)
-        both = keep.astype(F32) + got.astype(F32)
-        if d == 0:
-            both = base + both
-        else:
-            both = shift(both.astype(BF), "x", d).astype(F32)
-        arrived[d] = both
-    return arrived[0] + arrived[1] + arrived[2] + arrived[3]
+        return part(d, core).astype(F32) + got.astype(F32)
+
+    return both
+
+
+def send(a, by):
+    return shift(a.astype(BF), "x", by).astype(F32)
+
+
+def sum_at_owner(part, base):
+    both = halves_of(part)
+    arrived = [send(both(d), d) for d in (2, 1, 3)]
+    return base + both(0) + arrived[0] + arrived[1] + arrived[2]
+
+
+def sum_by_neighbours(part, base):
+    both = halves_of(part)
+    half = base.shape[0] // 2
+    across = both(2)
+    above = send(across[:half], 1)
+    below = send(across[half:], 3)
+    up = both(1)
+    up_lower = send(up[half:], 1)
+    down = both(3)
+    down_upper = send(down[:half], 3)
+    up_upper = send(up[:half] + above, 1)
+    down_lower = send(down[half:] + below, 3)
+    own = base + both(0)
+    return jnp.concatenate([own[:half] + up_upper + down_upper, own[half:] + up_lower + down_lower])
 
 
 def earlier_blocks(state, fillers):
@@ -341,7 +357,7 @@
         w = lax.dynamic_slice_in_dim(downs, at, W, 0)
         return dot(hidden, w, ((1,), (1,))).astype(BF)
 
-    return sum_at_owner(mlp, resid).astype(BF)
+    return sum_by_neighbours(mlp, resid).astype(BF)
 
 
 def solution(mesh):

time: 181 us -> 178 us (0.983)
  waiting for transfers between devices: 78.2 us -> 70.7 us
  starting transfers between devices: 50.5 us -> 54.4 us
    ppermute x34 -> x37, waiting for transfers between devices: 69.3 us -> 59.1 us  [shift(): return lax.ppermute(a, axis, [(i, (i + by) % n) for i in range(n)])]
    ppermute x34 -> x37, starting transfers between devices: 48.9 us -> 52.7 us  [shift(): return lax.ppermute(a, axis, [(i, (i + by) % n) for i in range(n)])]
    all_gather x1, waiting for transfers between devices: 6.07 us -> 8.68 us  [body(): weights = lax.all_gather(packed, SEQ, axis=0, tiled=True)]
  transfers between devices with their start and end apart: 36 -> 39, of which waited for: 18 -> 17; matrix products, arithmetic and copies ran while one was open for 4% -> 4% of each run, Pallas kernels for 7% -> 7%
where the time goes in v2:
time: 178 us; the launch traced here: 176 us
  waiting for transfers between devices  70.7 us (40%)
  starting transfers between devices  54.4 us (31%)
  Pallas kernels  23 us (13%)
  between operations  13.8 us (8%)
  matrix products  8.63 us (5%)
  other arithmetic  3.13 us (2%)
  local copies, waits for them, and re-layouts  2.84 us (2%)
    ppermute x37, waiting for transfers between devices, shift(): return lax.ppermute(a, axis, [(i, (i + by) % n) for i in range(n)])  59.1 us
    ppermute x37, starting transfers between devices, shift(): return lax.ppermute(a, axis, [(i, (i + by) % n) for i in range(n)])  52.7 us
    pallas_call x6, Pallas kernels, kernel_of(): pl.pallas_call(body, in_specs=specs, out_specs=[stays if space else vmem...  23 us
    all_gather x1, waiting for transfers between devices, body(): weights = lax.all_gather(packed, SEQ, axis=0, tiled=True)  8.68 us
    dot_general x16, matrix products, dot(): return lax.dot_general(a, b, (dims, ((), ())), preferred_element_type=F32)  8.63 us
  transfers between devices with their start and end apart: 39, of which 17 were waited for; matrix products, arithmetic and copies ran while one was open for 4% of the time, Pallas kernels for 7%

profile of v2, /device:TPU:1, one launch (start us, length us, event | category | flops | bytes accessed | tf_op | source)
XLA Modules:
  0.0 176.4 jit_solution(17951255841713055092)
XLA Ops:
  6.5 1.9 %pad_maximum_fusion = bf16[64,3072]{1,0:T(8,128)(2,1)} fusion(bf16[64,1024]{1,0:T(8,128)(2,1)} %bitcast.23, bf16[64,1024]{1,0:T(8,128)(2,1)} %param.18, bf16[64,1024]{1,0:T(8,128)(2,1)} %param.17), kind=kLoop, calls=%fused_computation.61 | loop fusion | flops 1179648 | bytes 786432 | tf_op jit(solution)/shard_map/concatenate | solution.py:277
  8.5 3.4 %collective-permute-start.2 = (bf16[768,256]{1,0:T(8,128)(2,1)}, bf16[768,256]{1,0:T(8,128)(2,1)S(1)}, u32[]{:S(2)}, u32[]{:S(2)}) collective-permute-start(bf16[768,256]{1,0:T(8,128)(2,1)} %refs_0_.1), channel_id=1, source_target_pairs={{0,6},{2,0},{4,2},{6,4},{1,7},{3,1},{5,3},{7,5},{8,14},{10,8},{12,... | collective-permute-start | bytes 1179656 | tf_op jit(solution)/shard_map/ppermute | solution.py:22
  13.0 1.5 collective-permute-start.3
  14.5 8.4 %collective-permute-done.2.refs_3_ = bf16[768,256]{1,0:T(8,128)(2,1)S(1)} collective-permute-done((bf16[768,256]{1,0:T(8,128)(2,1)}, bf16[768,256]{1,0:T(8,128)(2,1)S(1)}, u32[]{:S(2)}, u32[]{:S(2)}) %collective-permute-start.2) | collective-permute-done | bytes 393248 | tf_op jit(solution)/shard_map/ppermute | solution.py:22
  22.9 7.0 %collective-permute-start.6 = (bf16[768,256]{1,0:T(8,128)(2,1)S(1)}, bf16[768,256]{1,0:T(8,128)(2,1)S(1)}, u32[]{:S(2)}, u32[]{:S(2)}) collective-permute-start(bf16[768,256]{1,0:T(8,128)(2,1)S(1)} %collective-permute-done.2.refs_3_), channel_id=1, source_target_pairs={{0,1},{1,0},{2,3},{3,2},{4,5},{5,4},{6,7},{7,6},{8,9},{9,8},{10,11... | collective-permute-start | bytes 1179656 | tf_op jit(solution)/shard_map/ppermute | solution.py:22
  29.9 3.2 %collective-permute-done.refs_1_ = bf16[768,256]{1,0:T(8,128)(2,1)S(1)} collective-permute-done((bf16[768,256]{1,0:T(8,128)(2,1)}, bf16[768,256]{1,0:T(8,128)(2,1)S(1)}, u32[]{:S(2)}, u32[]{:S(2)}) %collective-permute-start) | collective-permute-done | bytes 393248 | tf_op jit(solution)/shard_map/ppermute | solution.py:22
  36.0 5.0 %shard_map.100 = (bf16[768,2048]{1,0:T(8,128)(2,1)S(1)}, bf16[768,256]{1,0:T(8,128)(2,1)S(1)}, bf16[768,256]{1,0:T(8,128)(2,1)S(1)}, bf16[2,128,128]{2,1,0:T(8,128)(2,1)S(1)}) custom-call(s32[2]{0:T(128)S(1)} %pad_add_fusion.place, bf16[768,256]{1,0:T(8,128)(2,1)S(1)} %copy-done.2, bf16[768,256]{1,0:T(8,128)(2,1)S(1)} %collective-permute-done.refs_1_, ...), custom_call_target="tpu_custom_call" | custom-call | flops 1610612736 | bytes 8388608 | tf_op jit(solution)/shard_map/pallas_call | solution.py:57
  41.8 1.6 collective-permute-start.7
  43.4 2.9 %collective-permute-done.7 = bf16[2,128,128]{2,1,0:T(8,128)(2,1)S(1)} collective-permute-done((bf16[2,128,128]{2,1,0:T(8,128)(2,1)S(1)}, bf16[2,128,128]{2,1,0:T(8,128)(2,1)S(1)}, u32[]{:S(2)}, u32[]{:S(2)}) %collective-permute-start.7) | collective-permute-done | bytes 65568 | tf_op jit(solution)/shard_map/ppermute | solution.py:254
  46.4 6.2 %collective-permute-start.10 = (bf16[2,128,128]{2,1,0:T(8,128)(2,1)S(1)}, bf16[2,128,128]{2,1,0:T(8,128)(2,1)S(1)}, u32[]{:S(2)}, u32[]{:S(2)}) collective-permute-start(bf16[2,128,128]{2,1,0:T(8,128)(2,1)S(1)} %fusion.55), channel_id=1, source_target_pairs={{0,48},{8,56},{16,0},{24,8},{32,16},{40,24},{48,32},{56,40},{1,49}... | collective-permute-start | bytes 196616 | tf_op jit(solution)/shard_map/ppermute | solution.py:22
  52.5 4.0 %collective-permute-start.8 = (bf16[2,128,128]{2,1,0:T(8,128)(2,1)S(1)}, bf16[2,128,128]{2,1,0:T(8,128)(2,1)S(1)}, u32[]{:S(2)}, u32[]{:S(2)}) collective-permute-start(bf16[2,128,128]{2,1,0:T(8,128)(2,1)S(1)} %fusion.55), channel_id=1, source_target_pairs={{0,32},{8,40},{16,48},{24,56},{32,0},{40,8},{48,16},{56,24},{1,33}... | collective-permute-start | bytes 196616 | tf_op jit(solution)/shard_map/ppermute | solution.py:22
  58.1 2.8 %collective-permute-done.8 = bf16[2,128,128]{2,1,0:T(8,128)(2,1)S(1)} collective-permute-done((bf16[2,128,128]{2,1,0:T(8,128)(2,1)S(1)}, bf16[2,128,128]{2,1,0:T(8,128)(2,1)S(1)}, u32[]{:S(2)}, u32[]{:S(2)}) %collective-permute-start.8) | collective-permute-done | bytes 65568 | tf_op jit(solution)/shard_map/ppermute | solution.py:22
  61.0 2.9 %collective-permute-start.13 = (bf16[2,128,128]{2,1,0:T(8,128)(2,1)S(1)}, bf16[2,128,128]{2,1,0:T(8,128)(2,1)S(1)}, u32[]{:S(2)}, u32[]{:S(2)}) collective-permute-start(bf16[2,128,128]{2,1,0:T(8,128)(2,1)S(1)} %fusion.46), channel_id=1, source_target_pairs={{0,192},{64,0},{128,64},{192,128},{1,193},{65,1},{129,65},{193,129... | collective-permute-start | bytes 196616 | tf_op jit(solution)/shard_map/ppermute | solution.py:22
  63.8 1.9 %collective-permute-start.11 = (bf16[2,128,128]{2,1,0:T(8,128)(2,1)S(1)}, bf16[2,128,128]{2,1,0:T(8,128)(2,1)S(1)}, u32[]{:S(2)}, u32[]{:S(2)}) collective-permute-start(bf16[2,128,128]{2,1,0:T(8,128)(2,1)S(1)} %fusion.46), channel_id=1, source_target_pairs={{0,128},{64,192},{128,0},{192,64},{1,129},{65,193},{129,1},{193,65... | collective-permute-start | bytes 196616 | tf_op jit(solution)/shard_map/ppermute | solution.py:22
  66.7 1.9 %shard_map.102.inside = f32[768,256]{1,0:T(8,128)S(1)} custom-call(bf16[768,256]{1,0:T(8,128)(2,1)S(1)} %shard_map.101.query, bf16[768,256]{1,0:T(8,128)(2,1)S(1)} %copy-done.7, bf16[768,256]{1,0:T(8,128)(2,1)S(1)} %copy-done.9), custom_call_target="tpu_custom_call" | custom-call | flops 603979776 | bytes 8388608 | tf_op jit(solution)/shard_map/pallas_call | solution.py:57
  70.2 4.0 %collective-permute-start.14 = (bf16[768,256]{1,0:T(8,128)(2,1)S(1)}, bf16[768,256]{1,0:T(8,128)(2,1)}, u32[]{:S(2)}, u32[]{:S(2)}) collective-permute-start(bf16[768,256]{1,0:T(8,128)(2,1)S(1)} %convolution_convert_fusion.14), channel_id=1, source_target_pairs={{0,1},{1,0},{2,3},{3,2},{4,5},{5,4},{6,7},{7,6},{8,9},{9,8},{10,11... | collective-permute-start | bytes 1179656 | tf_op jit(solution)/shard_map/ppermute | solution.py:22
  78.2 1.9 %collective-permute-start.20 = (bf16[768,256]{1,0:T(8,128)(2,1)S(1)}, bf16[768,256]{1,0:T(8,128)(2,1)}, u32[]{:S(2)}, u32[]{:S(2)}) collective-permute-start(bf16[768,256]{1,0:T(8,128)(2,1)S(1)} %fusion.12), channel_id=1, source_target_pairs={{0,6},{2,0},{4,2},{6,4},{1,7},{3,1},{5,3},{7,5},{8,14},{10,8},{12,... | collective-permute-start | bytes 1179656 | tf_op jit(solution)/shard_map/ppermute | solution.py:22
  80.2 8.5 %collective-permute-done.16 = bf16[768,256]{1,0:T(8,128)(2,1)} collective-permute-done((bf16[768,256]{1,0:T(8,128)(2,1)S(1)}, bf16[768,256]{1,0:T(8,128)(2,1)}, u32[]{:S(2)}, u32[]{:S(2)}) %collective-permute-start.16) | collective-permute-done | bytes 393248 | tf_op jit(solution)/shard_map/ppermute | solution.py:22
  88.7 9.0 %collective-permute-done.18 = bf16[768,256]{1,0:T(8,128)(2,1)} collective-permute-done((bf16[768,256]{1,0:T(8,128)(2,1)S(1)}, bf16[768,256]{1,0:T(8,128)(2,1)}, u32[]{:S(2)}, u32[]{:S(2)}) %collective-permute-start.18) | collective-permute-done | bytes 393248 | tf_op jit(solution)/shard_map/ppermute | solution.py:22
  97.7 1.8 %fusion.73 = (bf16[768,256]{1,0:T(8,128)(2,1)S(1)}, f32[768,256]{1,0:T(8,128)S(1)}) fusion(bf16[768,256]{1,0:T(8,128)(2,1)} %collective-permute-done.20, bf16[768,256]{1,0:T(8,128)(2,1)} %collective-permute-done.18, bf16[768,256]{1,0:T(8,128)(2,1)} %collective-permute-done.16, bf16[768,256]{1,0:T(8,128)(2,1)} %collective-permute-done.14, ...), kind=kOutput, calls=%fused_computation.106 | convolution fusion | flops 103219200 | bytes 3670020 | tf_op jit(solution)/shard_map/dot_general | solution.py:69
  102.1 7.8 %collective-permute-done.23.refs_3_ = bf16[768,256]{1,0:T(8,128)(2,1)S(1)} collective-permute-done((bf16[768,256]{1,0:T(8,128)(2,1)S(1)}, bf16[768,256]{1,0:T(8,128)(2,1)S(1)}, u32[]{:S(2)}, u32[]{:S(2)}) %collective-permute-start.23) | collective-permute-done | bytes 393248 | tf_op jit(solution)/shard_map/ppermute | solution.py:22
  109.9 2.2 %collective-permute-start.27 = (bf16[768,256]{1,0:T(8,128)(2,1)S(1)}, bf16[768,256]{1,0:T(8,128)(2,1)S(1)}, u32[]{:S(2)}, u32[]{:S(2)}) collective-permute-start(bf16[768,256]{1,0:T(8,128)(2,1)S(1)} %collective-permute-done.23.refs_3_), channel_id=1, source_target_pairs={{0,1},{1,0},{2,3},{3,2},{4,5},{5,4},{6,7},{7,6},{8,9},{9,8},{10,11... | collective-permute-start | bytes 1179656 | tf_op jit(solution)/shard_map/ppermute | solution.py:22
  112.1 2.3 %collective-permute-start.26 = (bf16[768,256]{1,0:T(8,128)(2,1)S(1)}, bf16[768,256]{1,0:T(8,128)(2,1)S(1)}, u32[]{:S(2)}, u32[]{:S(2)}) collective-permute-start(bf16[768,256]{1,0:T(8,128)(2,1)S(1)} %collective-permute-done.22.refs_2_), channel_id=1, source_target_pairs={{0,1},{1,0},{2,3},{3,2},{4,5},{5,4},{6,7},{7,6},{8,9},{9,8},{10,11... | collective-permute-start | bytes 1179656 | tf_op jit(solution)/shard_map/ppermute | solution.py:22
  114.4 6.8 %collective-permute-done.21.refs_1_ = bf16[768,256]{1,0:T(8,128)(2,1)S(1)} collective-permute-done((bf16[768,256]{1,0:T(8,128)(2,1)S(1)}, bf16[768,256]{1,0:T(8,128)(2,1)S(1)}, u32[]{:S(2)}, u32[]{:S(2)}) %collective-permute-start.21) | collective-permute-done | bytes 393248 | tf_op jit(solution)/shard_map/ppermute | solution.py:22
  122.9 3.7 %shard_map.104 = (bf16[768,2048]{1,0:T(8,128)(2,1)}, f32[768,128]{1,0:T(8,128)}) custom-call(s32[2]{0:T(128)S(1)} %pad_add_fusion.place, bf16[768,256]{1,0:T(8,128)(2,1)S(1)} %get-tuple-element.33.refs_0_, bf16[768,256]{1,0:T(8,128)(2,1)S(1)} %collective-permute-done.21.refs_1_, bf16[768,256]{1,0:T(8,128)(2,1)S(1)} %collective-permute-done.22.refs_2_, ...), custom_call_target="tpu_custom_call" | custom-call | flops 6291456 | bytes 8388608 | tf_op jit(solution)/shard_map/pallas_call | solution.py:57
  126.6 8.7 %all-gather.2.cloned.1.call-done.weights = bf16[2048,3072]{1,0:T(8,128)(2,1)} async-done(((bf16[64,3072]{1,0:T(8,128)(2,1)}), bf16[2048,3072]{1,0:T(8,128)(2,1)}) %all-gather.2.cloned.1.call-update) | async-done | bytes 12582928 | tf_op jit(solution)/shard_map/all_gather | solution.py:278
  135.2 10.1 %shard_map.105 = (bf16[768,1024]{1,0:T(8,128)(2,1)S(1)}, bf16[2048,1024]{1,0:T(8,128)(2,1)S(1)}) custom-call(bf16[768,2048]{1,0:T(8,128)(2,1)} %get-tuple-element.25.scaled_from, f32[768,128]{1,0:T(8,128)} %get-tuple-element.26.factor_from, bf16[2048,3072]{1,0:T(8,128)(2,1)} %all-gather.2.cloned.1.call-done.weights), custom_call_target="tpu_custom_call" | custom-call | flops 6442450944 | bytes 8388608 | tf_op jit(solution)/shard_map/pallas_call | solution.py:57
  152.2 2.0 %collective-permute-start.36 = (bf16[384,256]{1,0:T(8,128)(2,1)S(1)}, bf16[384,256]{1,0:T(8,128)(2,1)S(1)}, u32[]{:S(2)}, u32[]{:S(2)}) collective-permute-start(bf16[384,256]{1,0:T(8,128)(2,1)S(1)} %get-tuple-element.32), channel_id=1, source_target_pairs={{0,6},{2,0},{4,2},{6,4},{1,7},{3,1},{5,3},{7,5},{8,14},{10,8},{12,... | collective-permute-start | bytes 589832 | tf_op jit(solution)/shard_map/ppermute | solution.py:22
  154.8 1.4 collective-permute-start.34
  156.3 5.9 %collective-permute-done.31 = bf16[384,256]{1,0:T(8,128)(2,1)S(1)} collective-permute-done((bf16[384,256]{1,0:T(8,128)(2,1)S(1)}, bf16[384,256]{1,0:T(8,128)(2,1)S(1)}, u32[]{:S(2)}, u32[]{:S(2)}) %collective-permute-start.31) | collective-permute-done | bytes 196640 | tf_op jit(solution)/shard_map/ppermute | solution.py:22
  162.3 2.7 %collective-permute-start.37 = (bf16[384,256]{1,0:T(8,128)(2,1)S(1)}, bf16[384,256]{1,0:T(8,128)(2,1)S(1)}, u32[]{:S(2)}, u32[]{:S(2)}) collective-permute-start(bf16[384,256]{1,0:T(8,128)(2,1)S(1)} %fusion.33), channel_id=1, source_target_pairs={{0,6},{2,0},{4,2},{6,4},{1,7},{3,1},{5,3},{7,5},{8,14},{10,8},{12,... | collective-permute-start | bytes 589832 | tf_op jit(solution)/shard_map/ppermute | solution.py:22
  165.7 3.0 %collective-permute-done.32 = bf16[384,256]{1,0:T(8,128)(2,1)S(1)} collective-permute-done((bf16[384,256]{1,0:T(8,128)(2,1)S(1)}, bf16[384,256]{1,0:T(8,128)(2,1)S(1)}, u32[]{:S(2)}, u32[]{:S(2)}) %collective-permute-start.32) | collective-permute-done | bytes 196640 | tf_op jit(solution)/shard_map/ppermute | solution.py:22
  (101 shorter events, 26.2 us)
Async XLA Ops:
  6.5 128.7 %all-gather.2.cloned.1.call-start = ((), (), s32[]{:S(2)}) async-start(), calls=%async_computation | async-start | bytes 12976128 | tf_op jit(solution)/shard_map/all_gather | solution.py:278
  8.5 14.4 %collective-permute-start.2 = (bf16[768,256]{1,0:T(8,128)(2,1)}, bf16[768,256]{1,0:T(8,128)(2,1)S(1)}, u32[]{:S(2)}, u32[]{:S(2)}) collective-permute-start(bf16[768,256]{1,0:T(8,128)(2,1)} %refs_0_.1), channel_id=1, source_target_pairs={{0,6},{2,0},{4,2},{6,4},{1,7},{3,1},{5,3},{7,5},{8,14},{10,8},{12,... | collective-permute-start | bytes 1179656 | tf_op jit(solution)/shard_map/ppermute | solution.py:22
  11.8 18.1 %collective-permute-start.1 = (bf16[768,256]{1,0:T(8,128)(2,1)}, bf16[768,256]{1,0:T(8,128)(2,1)S(1)}, u32[]{:S(2)}, u32[]{:S(2)}) collective-permute-start(bf16[768,256]{1,0:T(8,128)(2,1)} %refs_0_.1), channel_id=1, source_target_pairs={{0,4},{2,6},{4,0},{6,2},{1,5},{3,7},{5,1},{7,3},{8,12},{10,14},{12... | collective-permute-start | bytes 1179656 | tf_op jit(solution)/shard_map/ppermute | solution.py:22
  12.4 20.8 %collective-permute-start = (bf16[768,256]{1,0:T(8,128)(2,1)}, bf16[768,256]{1,0:T(8,128)(2,1)S(1)}, u32[]{:S(2)}, u32[]{:S(2)}) collective-permute-start(bf16[768,256]{1,0:T(8,128)(2,1)} %refs_0_.1), channel_id=1, source_target_pairs={{0,2},{2,4},{4,6},{6,0},{1,3},{3,5},{5,7},{7,1},{8,10},{10,12},{12... | collective-permute-start | bytes 1179656 | tf_op jit(solution)/shard_map/ppermute | solution.py:22
  13.0 20.6 %collective-permute-start.3 = (bf16[768,256]{1,0:T(8,128)(2,1)}, bf16[768,256]{1,0:T(8,128)(2,1)S(1)}, u32[]{:S(2)}, u32[]{:S(2)}) collective-permute-start(bf16[768,256]{1,0:T(8,128)(2,1)} %refs_0_.1), channel_id=1, source_target_pairs={{0,1},{1,0},{2,3},{3,2},{4,5},{5,4},{6,7},{7,6},{8,9},{9,8},{10,11... | collective-permute-start | bytes 1179656 | tf_op jit(solution)/shard_map/ppermute | solution.py:22
  22.9 10.7 %collective-permute-start.6 = (bf16[768,256]{1,0:T(8,128)(2,1)S(1)}, bf16[768,256]{1,0:T(8,128)(2,1)S(1)}, u32[]{:S(2)}, u32[]{:S(2)}) collective-permute-start(bf16[768,256]{1,0:T(8,128)(2,1)S(1)} %collective-permute-done.2.refs_3_), channel_id=1, source_target_pairs={{0,1},{1,0},{2,3},{3,2},{4,5},{5,4},{6,7},{7,6},{8,9},{9,8},{10,11... | collective-permute-start | bytes 1179656 | tf_op jit(solution)/shard_map/ppermute | solution.py:22
  29.9 3.7 %collective-permute-start.5 = (bf16[768,256]{1,0:T(8,128)(2,1)S(1)}, bf16[768,256]{1,0:T(8,128)(2,1)S(1)}, u32[]{:S(2)}, u32[]{:S(2)}) collective-permute-start(bf16[768,256]{1,0:T(8,128)(2,1)S(1)} %collective-permute-done.1.refs_2_), channel_id=1, source_target_pairs={{0,1},{1,0},{2,3},{3,2},{4,5},{5,4},{6,7},{7,6},{8,9},{9,8},{10,11... | collective-permute-start | bytes 1179656 | tf_op jit(solution)/shard_map/ppermute | solution.py:22
  41.8 4.5 %collective-permute-start.7 = (bf16[2,128,128]{2,1,0:T(8,128)(2,1)S(1)}, bf16[2,128,128]{2,1,0:T(8,128)(2,1)S(1)}, u32[]{:S(2)}, u32[]{:S(2)}) collective-permute-start(bf16[2,128,128]{2,1,0:T(8,128)(2,1)S(1)} %get-tuple-element.17), channel_id=1, source_target_pairs={{0,8},{8,0},{16,24},{24,16},{32,40},{40,32},{48,56},{56,48},{1,9},... | collective-permute-start | bytes 196616 | tf_op jit(solution)/shard_map/ppermute | solution.py:254
  46.4 11.6 %collective-permute-start.10 = (bf16[2,128,128]{2,1,0:T(8,128)(2,1)S(1)}, bf16[2,128,128]{2,1,0:T(8,128)(2,1)S(1)}, u32[]{:S(2)}, u32[]{:S(2)}) collective-permute-start(bf16[2,128,128]{2,1,0:T(8,128)(2,1)S(1)} %fusion.55), channel_id=1, source_target_pairs={{0,48},{8,56},{16,0},{24,8},{32,16},{40,24},{48,32},{56,40},{1,49}... | collective-permute-start | bytes 196616 | tf_op jit(solution)/shard_map/ppermute | solution.py:22
  52.5 5.6 %collective-permute-start.9 = (bf16[2,128,128]{2,1,0:T(8,128)(2,1)S(1)}, bf16[2,128,128]{2,1,0:T(8,128)(2,1)S(1)}, u32[]{:S(2)}, u32[]{:S(2)}) collective-permute-start(bf16[2,128,128]{2,1,0:T(8,128)(2,1)S(1)} %fusion.55), channel_id=1, source_target_pairs={{0,16},{8,24},{16,32},{24,40},{32,48},{40,56},{48,0},{56,8},{1,17}... | collective-permute-start | bytes 196616 | tf_op jit(solution)/shard_map/ppermute | solution.py:22
  52.5 8.4 %collective-permute-start.8 = (bf16[2,128,128]{2,1,0:T(8,128)(2,1)S(1)}, bf16[2,128,128]{2,1,0:T(8,128)(2,1)S(1)}, u32[]{:S(2)}, u32[]{:S(2)}) collective-permute-start(bf16[2,128,128]{2,1,0:T(8,128)(2,1)S(1)} %fusion.55), channel_id=1, source_target_pairs={{0,32},{8,40},{16,48},{24,56},{32,0},{40,8},{48,16},{56,24},{1,33}... | collective-permute-start | bytes 196616 | tf_op jit(solution)/shard_map/ppermute | solution.py:22
  61.0 7.6 %collective-permute-start.13 = (bf16[2,128,128]{2,1,0:T(8,128)(2,1)S(1)}, bf16[2,128,128]{2,1,0:T(8,128)(2,1)S(1)}, u32[]{:S(2)}, u32[]{:S(2)}) collective-permute-start(bf16[2,128,128]{2,1,0:T(8,128)(2,1)S(1)} %fusion.46), channel_id=1, source_target_pairs={{0,192},{64,0},{128,64},{192,128},{1,193},{65,1},{129,65},{193,129... | collective-permute-start | bytes 196616 | tf_op jit(solution)/shard_map/ppermute | solution.py:22
  63.8 5.0 %collective-permute-start.12 = (bf16[2,128,128]{2,1,0:T(8,128)(2,1)S(1)}, bf16[2,128,128]{2,1,0:T(8,128)(2,1)S(1)}, u32[]{:S(2)}, u32[]{:S(2)}) collective-permute-start(bf16[2,128,128]{2,1,0:T(8,128)(2,1)S(1)} %fusion.46), channel_id=1, source_target_pairs={{0,64},{64,128},{128,192},{192,0},{1,65},{65,129},{129,193},{193,1... | collective-permute-start | bytes 196616 | tf_op jit(solution)/shard_map/ppermute | solution.py:22
  63.8 5.0 %collective-permute-start.11 = (bf16[2,128,128]{2,1,0:T(8,128)(2,1)S(1)}, bf16[2,128,128]{2,1,0:T(8,128)(2,1)S(1)}, u32[]{:S(2)}, u32[]{:S(2)}) collective-permute-start(bf16[2,128,128]{2,1,0:T(8,128)(2,1)S(1)} %fusion.46), channel_id=1, source_target_pairs={{0,128},{64,192},{128,0},{192,64},{1,129},{65,193},{129,1},{193,65... | collective-permute-start | bytes 196616 | tf_op jit(solution)/shard_map/ppermute | solution.py:22
  70.2 10.0 %collective-permute-start.14 = (bf16[768,256]{1,0:T(8,128)(2,1)S(1)}, bf16[768,256]{1,0:T(8,128)(2,1)}, u32[]{:S(2)}, u32[]{:S(2)}) collective-permute-start(bf16[768,256]{1,0:T(8,128)(2,1)S(1)} %convolution_convert_fusion.14), channel_id=1, source_target_pairs={{0,1},{1,0},{2,3},{3,2},{4,5},{5,4},{6,7},{7,6},{8,9},{9,8},{10,11... | collective-permute-start | bytes 1179656 | tf_op jit(solution)/shard_map/ppermute | solution.py:22
  76.5 12.2 %collective-permute-start.16 = (bf16[768,256]{1,0:T(8,128)(2,1)S(1)}, bf16[768,256]{1,0:T(8,128)(2,1)}, u32[]{:S(2)}, u32[]{:S(2)}) collective-permute-start(bf16[768,256]{1,0:T(8,128)(2,1)S(1)} %fusion.18), channel_id=1, source_target_pairs={{0,4},{2,6},{4,0},{6,2},{1,5},{3,7},{5,1},{7,3},{8,12},{10,14},{12... | collective-permute-start | bytes 1179656 | tf_op jit(solution)/shard_map/ppermute | solution.py:22
  77.1 20.6 %collective-permute-start.18 = (bf16[768,256]{1,0:T(8,128)(2,1)S(1)}, bf16[768,256]{1,0:T(8,128)(2,1)}, u32[]{:S(2)}, u32[]{:S(2)}) collective-permute-start(bf16[768,256]{1,0:T(8,128)(2,1)S(1)} %fusion.15), channel_id=1, source_target_pairs={{0,2},{2,4},{4,6},{6,0},{1,3},{3,5},{5,7},{7,1},{8,10},{10,12},{12... | collective-permute-start | bytes 1179656 | tf_op jit(solution)/shard_map/ppermute | solution.py:22
  78.2 19.4 %collective-permute-start.20 = (bf16[768,256]{1,0:T(8,128)(2,1)S(1)}, bf16[768,256]{1,0:T(8,128)(2,1)}, u32[]{:S(2)}, u32[]{:S(2)}) collective-permute-start(bf16[768,256]{1,0:T(8,128)(2,1)S(1)} %fusion.12), channel_id=1, source_target_pairs={{0,6},{2,0},{4,2},{6,4},{1,7},{3,1},{5,3},{7,5},{8,14},{10,8},{12,... | collective-permute-start | bytes 1179656 | tf_op jit(solution)/shard_map/ppermute | solution.py:22
  99.5 10.4 %collective-permute-start.23 = (bf16[768,256]{1,0:T(8,128)(2,1)S(1)}, bf16[768,256]{1,0:T(8,128)(2,1)S(1)}, u32[]{:S(2)}, u32[]{:S(2)}) collective-permute-start(bf16[768,256]{1,0:T(8,128)(2,1)S(1)} %get-tuple-element.33.refs_0_), channel_id=1, source_target_pairs={{0,6},{2,0},{4,2},{6,4},{1,7},{3,1},{5,3},{7,5},{8,14},{10,8},{12,... | collective-permute-start | bytes 1179656 | tf_op jit(solution)/shard_map/ppermute | solution.py:22
  100.1 12.0 %collective-permute-start.22 = (bf16[768,256]{1,0:T(8,128)(2,1)S(1)}, bf16[768,256]{1,0:T(8,128)(2,1)S(1)}, u32[]{:S(2)}, u32[]{:S(2)}) collective-permute-start(bf16[768,256]{1,0:T(8,128)(2,1)S(1)} %get-tuple-element.33.refs_0_), channel_id=1, source_target_pairs={{0,4},{2,6},{4,0},{6,2},{1,5},{3,7},{5,1},{7,3},{8,12},{10,14},{12... | collective-permute-start | bytes 1179656 | tf_op jit(solution)/shard_map/ppermute | solution.py:22
  100.1 21.1 %collective-permute-start.21 = (bf16[768,256]{1,0:T(8,128)(2,1)S(1)}, bf16[768,256]{1,0:T(8,128)(2,1)S(1)}, u32[]{:S(2)}, u32[]{:S(2)}) collective-permute-start(bf16[768,256]{1,0:T(8,128)(2,1)S(1)} %get-tuple-element.33.refs_0_), channel_id=1, source_target_pairs={{0,2},{2,4},{4,6},{6,0},{1,3},{3,5},{5,7},{7,1},{8,10},{10,12},{12... | collective-permute-start | bytes 1179656 | tf_op jit(solution)/shard_map/ppermute | solution.py:22
  101.1 20.5 %collective-permute-start.24 = (bf16[768,256]{1,0:T(8,128)(2,1)S(1)}, bf16[768,256]{1,0:T(8,128)(2,1)S(1)}, u32[]{:S(2)}, u32[]{:S(2)}) collective-permute-start(bf16[768,256]{1,0:T(8,128)(2,1)S(1)} %get-tuple-element.33.refs_0_), channel_id=1, source_target_pairs={{0,1},{1,0},{2,3},{3,2},{4,5},{5,4},{6,7},{7,6},{8,9},{9,8},{10,11... | collective-permute-start | bytes 1179656 | tf_op jit(solution)/shard_map/ppermute | solution.py:22
  109.9 11.6 %collective-permute-start.27 = (bf16[768,256]{1,0:T(8,128)(2,1)S(1)}, bf16[768,256]{1,0:T(8,128)(2,1)S(1)}, u32[]{:S(2)}, u32[]{:S(2)}) collective-permute-start(bf16[768,256]{1,0:T(8,128)(2,1)S(1)} %collective-permute-done.23.refs_3_), channel_id=1, source_target_pairs={{0,1},{1,0},{2,3},{3,2},{4,5},{5,4},{6,7},{7,6},{8,9},{9,8},{10,11... | collective-permute-start | bytes 1179656 | tf_op jit(solution)/shard_map/ppermute | solution.py:22
  112.1 9.5 %collective-permute-start.26 = (bf16[768,256]{1,0:T(8,128)(2,1)S(1)}, bf16[768,256]{1,0:T(8,128)(2,1)S(1)}, u32[]{:S(2)}, u32[]{:S(2)}) collective-permute-start(bf16[768,256]{1,0:T(8,128)(2,1)S(1)} %collective-permute-done.22.refs_2_), channel_id=1, source_target_pairs={{0,1},{1,0},{2,3},{3,2},{4,5},{5,4},{6,7},{7,6},{8,9},{9,8},{10,11... | collective-permute-start | bytes 1179656 | tf_op jit(solution)/shard_map/ppermute | solution.py:22
  149.2 15.8 %collective-permute-start.28 = (bf16[768,256]{1,0:T(8,128)(2,1)S(1)}, bf16[768,256]{1,0:T(8,128)(2,1)S(1)}, u32[]{:S(2)}, u32[]{:S(2)}) collective-permute-start(bf16[768,256]{1,0:T(8,128)(2,1)S(1)} %convolution_convert_fusion.6), channel_id=1, source_target_pairs={{0,1},{1,0},{2,3},{3,2},{4,5},{5,4},{6,7},{7,6},{8,9},{9,8},{10,11... | collective-permute-start | bytes 1179656 | tf_op jit(solution)/shard_map/ppermute | solution.py:22
  149.8 4.3 %collective-permute-start.33 = (bf16[768,256]{1,0:T(8,128)(2,1)S(1)}, bf16[768,256]{1,0:T(8,128)(2,1)S(1)}, u32[]{:S(2)}, u32[]{:S(2)}) collective-permute-start(bf16[768,256]{1,0:T(8,128)(2,1)S(1)} %convolution_convert_fusion), channel_id=1, source_target_pairs={{0,1},{1,0},{2,3},{3,2},{4,5},{5,4},{6,7},{7,6},{8,9},{9,8},{10,11... | collective-permute-start | bytes 1179656 | tf_op jit(solution)/shard_map/ppermute | solution.py:22
  150.6 15.1 %collective-permute-start.35 = (bf16[384,256]{1,0:T(8,128)(2,1)S(1)}, bf16[384,256]{1,0:T(8,128)(2,1)S(1)}, u32[]{:S(2)}, u32[]{:S(2)}) collective-permute-start(bf16[384,256]{1,0:T(8,128)(2,1)S(1)} %slice.62), channel_id=1, source_target_pairs={{0,2},{2,4},{4,6},{6,0},{1,3},{3,5},{5,7},{7,1},{8,10},{10,12},{12... | collective-permute-start | bytes 589832 | tf_op jit(solution)/shard_map/ppermute | solution.py:22
  151.3 10.8 %collective-permute-start.31 = (bf16[384,256]{1,0:T(8,128)(2,1)S(1)}, bf16[384,256]{1,0:T(8,128)(2,1)S(1)}, u32[]{:S(2)}, u32[]{:S(2)}) collective-permute-start(bf16[384,256]{1,0:T(8,128)(2,1)S(1)} %get-tuple-element.31), channel_id=1, source_target_pairs={{0,2},{2,4},{4,6},{6,0},{1,3},{3,5},{5,7},{7,1},{8,10},{10,12},{12... | collective-permute-start | bytes 589832 | tf_op jit(solution)/shard_map/ppermute | solution.py:22
  152.2 10.1 %collective-permute-start.36 = (bf16[384,256]{1,0:T(8,128)(2,1)S(1)}, bf16[384,256]{1,0:T(8,128)(2,1)S(1)}, u32[]{:S(2)}, u32[]{:S(2)}) collective-permute-start(bf16[384,256]{1,0:T(8,128)(2,1)S(1)} %get-tuple-element.32), channel_id=1, source_target_pairs={{0,6},{2,0},{4,2},{6,4},{1,7},{3,1},{5,3},{7,5},{8,14},{10,8},{12,... | collective-permute-start | bytes 589832 | tf_op jit(solution)/shard_map/ppermute | solution.py:22
  154.8 10.9 %collective-permute-start.34 = (bf16[384,256]{1,0:T(8,128)(2,1)S(1)}, bf16[384,256]{1,0:T(8,128)(2,1)S(1)}, u32[]{:S(2)}, u32[]{:S(2)}) collective-permute-start(bf16[384,256]{1,0:T(8,128)(2,1)S(1)} %slice.63), channel_id=1, source_target_pairs={{0,6},{2,0},{4,2},{6,4},{1,7},{3,1},{5,3},{7,5},{8,14},{10,8},{12,... | collective-permute-start | bytes 589832 | tf_op jit(solution)/shard_map/ppermute | solution.py:22
  162.2 6.5 %collective-permute-start.32 = (bf16[384,256]{1,0:T(8,128)(2,1)S(1)}, bf16[384,256]{1,0:T(8,128)(2,1)S(1)}, u32[]{:S(2)}, u32[]{:S(2)}) collective-permute-start(bf16[384,256]{1,0:T(8,128)(2,1)S(1)} %fusion.36), channel_id=1, source_target_pairs={{0,2},{2,4},{4,6},{6,0},{1,3},{3,5},{5,7},{7,1},{8,10},{10,12},{12... | collective-permute-start | bytes 589832 | tf_op jit(solution)/shard_map/ppermute | solution.py:22
  162.3 6.3 %collective-permute-start.37 = (bf16[384,256]{1,0:T(8,128)(2,1)S(1)}, bf16[384,256]{1,0:T(8,128)(2,1)S(1)}, u32[]{:S(2)}, u32[]{:S(2)}) collective-permute-start(bf16[384,256]{1,0:T(8,128)(2,1)S(1)} %fusion.33), channel_id=1, source_target_pairs={{0,6},{2,0},{4,2},{6,4},{1,7},{3,1},{5,3},{7,5},{8,14},{10,8},{12,... | collective-permute-start | bytes 589832 | tf_op jit(solution)/shard_map/ppermute | solution.py:22
  (17 other events, 204.4 us)
Sparse Core Ops, SparseCore 0:
  9.9 125.2 all-gather.1
